TPU v7x, 32 devices: a whole 2x2x4 slice. The times are simulated.
32 devices in a mesh: gx: 2 (over x), gy: 4 (over z), gz: 4 (over y, core).
Axes of the slice: x: 2, y: 2, z: 4, core: 2. Of those that a mesh axis runs over, the one named last changes fastest.
Arguments:
- offsets: float32 [3, 4, 8, 8, 128], P(None, 'gx', 'gy', 'gz'), may hold values from 0 to 1
- masses: float32 [4, 8, 8, 128], P('gx', 'gy', 'gz'), may hold values from 0.12 to 3
- smoothing: float32 [4, 8, 8, 128], P('gx', 'gy', 'gz'), may hold values from 0.6 to 0.75
- velocity: float32 [3, 4, 8, 8, 128], P(None, 'gx', 'gy', 'gz'), may hold values from -6 to 6
- energy: float32 [4, 8, 8, 128], P('gx', 'gy', 'gz'), may hold values from 0.3 to 3
- active: int32 [4, 8, 8, 128], P('gx', 'gy', 'gz'), may hold values from 0 to 1, as said below
Outputs:
- density: float32 [4, 8, 8, 128], P('gx', 'gy', 'gz')
- acceleration: float32 [3, 4, 8, 8, 128], P(None, 'gx', 'gy', 'gz')
- heating: float32 [4, 8, 8, 128], P('gx', 'gy', 'gz')
Inputs may be any that keep to these rules, and one draw needn't show every extreme that they name: The share of active particles differs from cell to cell, from none to all.
All inputs are finite; a program needn't handle non-finite values.
Results may differ from a plain program's by a relative error of at most 0.0003.
Values sent between devices are 32-bit elements; how exact they have to be, the bound alone decides.
No kernel may reach another device: no remote copies, remote signals or barrier semaphores. Data moves between devices by JAX's collectives and lax.ppermute only.
A program may use at most 64 MiB of HBM per device.

v0:
```python
import functools

import jax
import jax.numpy as jnp
from jax import lax
from jax.experimental import pallas as pl
from jax.experimental.pallas import tpu as pltpu
from jax.sharding import PartitionSpec as P

PASSES = 2

kernel_norm = 2.5464790894703255
eta_factor = 2.3
gamma_index = 5.0 / 3.0

ROWS = 32
TINY = 1e-12
AXES = ("gx", "gy", "gz")


def ring(axis, step):
    count = lax.axis_size(axis)
    return [(i, (i + step) % count) for i in range(count)]


def halo(block):
    for dim, axis in enumerate(AXES):
        size = block.shape[dim]
        if lax.axis_size(axis) == 2:
            other = lax.ppermute(block, axis, ring(axis, 1))
            low = lax.slice_in_dim(other, size - 1, size, axis=dim)
            high = lax.slice_in_dim(other, 0, 1, axis=dim)
        else:
            low = lax.ppermute(
                lax.slice_in_dim(block, size - 1, size, axis=dim), axis, ring(axis, 1)
            )
            high = lax.ppermute(lax.slice_in_dim(block, 0, 1, axis=dim), axis, ring(axis, -1))
        block = jnp.concatenate([low, block, high], axis=dim)
    return block


def cube_root(value):
    return jnp.exp(jnp.log(value) * (1.0 / 3.0))


def split3(value):
    high = value.astype(jnp.bfloat16).astype(jnp.float32)
    rest = value - high
    mid = rest.astype(jnp.bfloat16).astype(jnp.float32)
    return high, mid, rest - mid


def row_index():
    return lax.broadcasted_iota(jnp.int32, (8, 128), 0)


def place(fields, origin):
    row = row_index()
    shift = jnp.where(row == 0, origin[0], jnp.where(row == 1, origin[1], origin[2]))
    spot = jnp.where(row < 3, fields + shift, 0.0)
    return spot, jnp.sum(spot * spot, axis=0, keepdims=True)


def source_rows(spot, square, scale):
    row = row_index()
    value = jnp.where(row == 3, square, jnp.where(row == 4, 1.0, spot)) * scale
    high, mid, low = split3(value)
    return jnp.concatenate([high, mid, high, mid, low, high], axis=0)


def target_rows(spot, square, scale):
    row = row_index()
    value = jnp.where(row == 3, 1.0, jnp.where(row == 4, square, -2.0 * spot)) * scale
    high, mid, low = split3(value)
    return jnp.concatenate([high, high, mid, mid, high, low], axis=0)


def weights_of(value):
    high, mid, low = split3(value)
    rows = jnp.concatenate([high, mid, low, jnp.zeros_like(low)], axis=0)
    return jnp.concatenate([rows, rows], axis=1).astype(jnp.bfloat16)


def product(left, right):
    return jnp.dot(left, right, preferred_element_type=jnp.float32)


def tiled(rows, count):
    return jnp.concatenate([rows] * count, axis=0)


def origin_of(cell, sizes):
    return [c - 0.5 * n for c, n in zip(cell, sizes)]


def cells_of(sizes):
    return [(x, y, z) for x in range(sizes[0]) for y in range(sizes[1]) for z in range(sizes[2])]


def density_kernel(src_ref, len_ref, rho_ref, r_ref, c_ref, *, sizes):
    nx, ny, nz = sizes
    cx, cy, cz = nx - 2, ny - 2, nz - 2
    for x, y, z in cells_of(sizes):
        fields = src_ref[x, y, z]
        spot, square = place(fields, origin_of((x, y, z), sizes))
        root = cube_root(fields[3:4])
        r_ref[x * ny + y, :, z * 128 : (z + 1) * 128] = source_rows(
            spot, square, root * root
        ).astype(jnp.bfloat16)
        c_ref[x * ny + y, :, z * 128 : (z + 1) * 128] = jnp.broadcast_to(root, (8, 128))

    def one_cell(index, carry):
        x = index // (cy * cz)
        y = index // cz % cy
        z = index % cz
        fields = src_ref[x + 1, y + 1, z + 1]
        where = [v.astype(jnp.float32) + (1.0 - 0.5 * n) for v, n in zip((x, y, z), sizes)]
        spot, square = place(fields, where)
        length = len_ref[x, y, pl.ds(z, 1), :]
        lanes = pl.ds(pl.multiple_of(z * 128, 128), 384)
        for pass_index in range(PASSES):
            inverse = 1.0 / length
            left = target_rows(spot, square, inverse * inverse).T.astype(jnp.bfloat16)
            sums = []
            for first in range(0, 128, ROWS):
                near = jnp.zeros((ROWS, 128), jnp.float32)
                far = jnp.zeros((ROWS, 128), jnp.float32)
                for dx in range(3):
                    for dy in range(3):
                        line = (x + dx) * ny + y + dy
                        s = product(left[first : first + ROWS], r_ref[line, :, lanes])
                        root = tiled(c_ref[line, :, lanes], ROWS // 8)
                        s = jnp.maximum(s, TINY)
                        scaled = s * lax.rsqrt(s)
                        t = root - scaled
                        a = jnp.maximum(t, 0.0)
                        b = jnp.maximum(t - scaled, 0.0)
                        a = a * a * a
                        b = b * b * b
                        for k in range(3):
                            far = far + a[:, k * 128 : (k + 1) * 128]
                            near = near + b[:, k * 128 : (k + 1) * 128]
                sums.append(2.0 * far - near)
            total = jnp.sum(jnp.concatenate(sums, axis=0).T, axis=0, keepdims=True)
            density = kernel_norm * total * (inverse * inverse * inverse)
            length = eta_factor * cube_root(fields[3:4] / density)
        rho_ref[x, y, pl.ds(z, 1), :] = density
        return carry

    lax.fori_loop(0, cx * cy * cz, one_cell, 0)


def profile(s):
    s = jnp.maximum(s, TINY)
    rs = lax.rsqrt(s)
    q = s * rs
    t = 1.0 - q
    a = jnp.maximum(t, 0.0)
    b = jnp.maximum(t - q, 0.0)
    g = jnp.minimum(a, q) * (a + b) * rs
    high = g.astype(jnp.bfloat16)
    low = (g - high.astype(jnp.float32)).astype(jnp.bfloat16)
    return jnp.concatenate([high, low], axis=0)


def own_basis(fields, spot):
    row = row_index()
    along = jnp.sum(fields[4:7] * spot[0:3], axis=0, keepdims=True)
    basis = jnp.where(row < 3, spot, jnp.where(row == 3, 1.0, fields))
    return jnp.where(row == 7, along, basis)


def smooth(fields, density):
    inverse = 1.0 / (eta_factor * cube_root(fields[3:4] / density))
    inv2 = inverse * inverse
    press = (gamma_index - 1.0) * fields[7:8] / density
    return inv2, press * (-6.0 * kernel_norm) * inv2 * inv2 * inverse


def gather_sums(right, point_ref, col_ref, x, y, z, ny):
    total = jnp.zeros((32, 128), jnp.float32)
    for dx in range(3):
        for dy in range(3):
            line = (x + dx) * ny + y + dy
            for dz in range(3):
                rows = pl.ds(pl.multiple_of((z + dz) * 128, 128), 128)
                lanes = pl.ds(pl.multiple_of((z + dz) * 256, 256), 256)
                g = profile(product(point_ref[line, rows, :], right))
                total = total + product(col_ref[line, :, lanes], g)
    return total[0:8] + total[8:16] + total[16:24]


def target_place(src_ref, x, y, z, sizes):
    fields = src_ref[x + 1, y + 1, z + 1]
    where = [v.astype(jnp.float32) + (1.0 - 0.5 * n) for v, n in zip((x, y, z), sizes)]
    spot, square = place(fields, where)
    return fields, spot, square


def own_kernel(src_ref, rho_ref, sum_ref, point_ref, col_ref, *, sizes):
    nx, ny, nz = sizes
    cx, cy, cz = nx - 2, ny - 2, nz - 2
    for x, y, z in cells_of(sizes):
        fields = src_ref[x, y, z]
        spot, square = place(fields, origin_of((x, y, z), sizes))
        line = x * ny + y
        point_ref[line, z * 128 : (z + 1) * 128, :] = source_rows(spot, square, 1.0).T.astype(
            jnp.bfloat16
        )
        col_ref[line, :, z * 256 : (z + 1) * 256] = weights_of(
            own_basis(fields, spot) * fields[3:4]
        )

    def one_cell(index, carry):
        x = index // (cy * cz)
        y = index // cz % cy
        z = index % cz
        fields, spot, square = target_place(src_ref, x, y, z, sizes)
        inv2, strength = smooth(fields, rho_ref[x, y, pl.ds(z, 1), :])
        right = target_rows(spot, square, inv2).astype(jnp.bfloat16)
        sum_ref[x, y, z] = gather_sums(right, point_ref, col_ref, x, y, z, ny) * strength
        return carry

    lax.fori_loop(0, cx * cy * cz, one_cell, 0)


def their_kernel(
    src_ref, rho_ref, sum_ref, act_ref, push_ref, heat_ref, point_ref, col_ref, *, sizes
):
    nx, ny, nz = sizes
    cx, cy, cz = nx - 2, ny - 2, nz - 2
    row = row_index()
    for x, y, z in cells_of(sizes):
        fields = src_ref[x, y, z]
        spot, square = place(fields, origin_of((x, y, z), sizes))
        inv2, strength = smooth(fields, rho_ref[x, y, z])
        line = x * ny + y
        point_ref[line, z * 128 : (z + 1) * 128, :] = source_rows(spot, square, inv2).T.astype(
            jnp.bfloat16
        )
        basis = jnp.where(row == 3, 1.0, spot)
        col_ref[line, :, z * 256 : (z + 1) * 256] = weights_of(basis * (fields[3:4] * strength))

    def one_cell(index, carry):
        x = index // (cy * cz)
        y = index // cz % cy
        z = index % cz
        fields, spot, square = target_place(src_ref, x, y, z, sizes)
        right = target_rows(spot, square, 1.0).astype(jnp.bfloat16)
        their = gather_sums(right, point_ref, col_ref, x, y, z, ny)
        own = sum_ref[x, y, z]
        active = act_ref[x, y, pl.ds(z, 1), :].astype(jnp.float32)
        spot = spot[0:3]
        push = spot * (own[3:4] + their[3:4]) - own[0:3] - their[0:3]
        heat = fields[4:7] * (spot * own[3:4] - own[0:3]) - spot * own[4:7]
        heat = jnp.sum(heat, axis=0, keepdims=True) + own[7:8]
        for k in range(3):
            push_ref[k, x, y, pl.ds(z, 1), :] = -active * push[k : k + 1]
        heat_ref[x, y, pl.ds(z, 1), :] = active * heat
        return carry

    lax.fori_loop(0, cx * cy * cz, one_cell, 0)


def body(offsets, masses, smoothing, velocity, energy, active):
    local = masses.shape[:3]
    sizes = tuple(n + 2 for n in local)
    nx, ny, nz = sizes
    f32 = jnp.float32
    static = jnp.stack(
        [offsets[0], offsets[1], offsets[2], masses, velocity[0], velocity[1], velocity[2], energy],
        axis=3,
    )
    padded = halo(static)
    density = pl.pallas_call(
        functools.partial(density_kernel, sizes=sizes),
        out_shape=jax.ShapeDtypeStruct(masses.shape, f32),
        scratch_shapes=[
            pltpu.VMEM((nx * ny, 48, nz * 128), jnp.bfloat16),
            pltpu.VMEM((nx * ny, 8, nz * 128), f32),
        ],
        name="density",
    )(padded, smoothing)
    imported = halo(density[..., None, :])
    tables = [
        pltpu.VMEM((nx * ny, nz * 128, 48), jnp.bfloat16),
        pltpu.VMEM((nx * ny, 32, nz * 256), jnp.bfloat16),
    ]
    sums = pl.pallas_call(
        functools.partial(own_kernel, sizes=sizes),
        out_shape=jax.ShapeDtypeStruct(static.shape, f32),
        scratch_shapes=tables,
        name="own",
    )(padded, density)
    push, heat = pl.pallas_call(
        functools.partial(their_kernel, sizes=sizes),
        out_shape=(
            jax.ShapeDtypeStruct((3,) + masses.shape, f32),
            jax.ShapeDtypeStruct(masses.shape, f32),
        ),
        scratch_shapes=tables,
        name="their",
    )(padded, imported, sums, active)
    return (density, push, heat)


def solution(mesh):
    vector = P(None, "gx", "gy", "gz", None)
    scalar = P("gx", "gy", "gz", None)
    return jax.shard_map(
        body,
        mesh=mesh,
        in_specs=(vector, scalar, scalar, vector, scalar, scalar),
        out_specs=(scalar, vector, scalar),
        check_vma=False,
    )
```

profile of v0, /device:TPU:0, one launch (start us, length us, event | category | flops | bytes accessed | tf_op | source)
XLA Modules:
  0.0 76.1 jit_solution(7298948808115840669)
XLA Ops:
  0.6 0.7 fusion.5
  1.4 0.0 copy-done.2
  1.4 0.0 copy-start.3
  1.4 0.7 copy-done.4
  2.1 0.0 copy-done.3
  2.1 0.1 stack.11
  2.1 3.0 %collective-permute-start = (f32[2,2,2,8,128]{4,3,2,1,0:T(8,128)S(1)}, f32[2,2,2,8,128]{4,3,2,1,0:T(8,128)S(1)}, u32[]{:S(2)}, u32[]{:S(2)}) collective-permute-start(f32[2,2,2,8,128]{4,3,2,1,0:T(8,128)S(1)} %stack.11), channel_id=1, source_target_pairs={{0,16},{16,0},{1,17},{17,1},{2,18},{18,2},{3,19},{19,3},{4,20},{20... | collective-permute-start | bytes 98312 | tf_op jit(solution)/shard_map/ppermute | solution.py:30
  5.2 1.9 %collective-permute-done = f32[2,2,2,8,128]{4,3,2,1,0:T(8,128)S(1)} collective-permute-done((f32[2,2,2,8,128]{4,3,2,1,0:T(8,128)S(1)}, f32[2,2,2,8,128]{4,3,2,1,0:T(8,128)S(1)}, u32[]{:S(2)}, u32[]{:S(2)}) %collective-permute-start) | collective-permute-done | bytes 32800 | tf_op jit(solution)/shard_map/ppermute | solution.py:30
  7.1 2.2 %collective-permute-start.1 = (f32[4,1,2,8,128]{4,3,2,1,0:T(8,128)S(1)}, f32[4,1,2,8,128]{4,3,2,1,0:T(8,128)S(1)}, u32[]{:S(2)}, u32[]{:S(2)}) collective-permute-start(f32[4,1,2,8,128]{4,3,2,1,0:T(8,128)S(1)} %get-tuple-element.9), channel_id=1, source_target_pairs={{0,4},{4,8},{8,12},{12,0},{1,5},{5,9},{9,13},{13,1},{2,6},{6,10},{... | collective-permute-start | bytes 98312 | tf_op jit(solution)/shard_map/ppermute | solution.py:34
  9.2 2.1 %collective-permute-start.2 = (f32[4,1,2,8,128]{4,3,2,1,0:T(8,128)S(1)}, f32[4,1,2,8,128]{4,3,2,1,0:T(8,128)S(1)}, u32[]{:S(2)}, u32[]{:S(2)}) collective-permute-start(f32[4,1,2,8,128]{4,3,2,1,0:T(8,128)S(1)} %get-tuple-element.10), channel_id=1, source_target_pairs={{0,12},{4,0},{8,4},{12,8},{1,13},{5,1},{9,5},{13,9},{2,14},{6,2},{... | collective-permute-start | bytes 98312 | tf_op jit(solution)/shard_map/ppermute | solution.py:37
  11.3 1.9 %collective-permute-done.1 = f32[4,1,2,8,128]{4,3,2,1,0:T(8,128)S(1)} collective-permute-done((f32[4,1,2,8,128]{4,3,2,1,0:T(8,128)S(1)}, f32[4,1,2,8,128]{4,3,2,1,0:T(8,128)S(1)}, u32[]{:S(2)}, u32[]{:S(2)}) %collective-permute-start.1) | collective-permute-done | bytes 32800 | tf_op jit(solution)/shard_map/ppermute | solution.py:34
  13.3 0.2 collective-permute-done.2
  13.5 0.1 collective-permute-start.3
  13.6 1.7 %collective-permute-start.4 = (f32[4,4,1,8,128]{4,3,2,1,0:T(8,128)S(1)}, f32[4,4,1,8,128]{4,3,2,1,0:T(8,128)S(1)}, u32[]{:S(2)}, u32[]{:S(2)}) collective-permute-start(f32[4,4,1,8,128]{4,3,2,1,0:T(8,128)S(1)} %get-tuple-element.8), channel_id=1, source_target_pairs={{0,3},{1,0},{2,1},{3,2},{4,7},{5,4},{6,5},{7,6},{8,11},{9,8},{10,9... | collective-permute-start | bytes 196616 | tf_op jit(solution)/shard_map/ppermute | solution.py:37
  15.3 1.9 %collective-permute-done.3 = f32[4,4,1,8,128]{4,3,2,1,0:T(8,128)S(1)} collective-permute-done((f32[4,4,1,8,128]{4,3,2,1,0:T(8,128)S(1)}, f32[4,4,1,8,128]{4,3,2,1,0:T(8,128)S(1)}, u32[]{:S(2)}, u32[]{:S(2)}) %collective-permute-start.3) | collective-permute-done | bytes 65568 | tf_op jit(solution)/shard_map/ppermute | solution.py:34
  17.3 0.0 collective-permute-done.4
  17.3 0.7 pad_maximum_fusion.src_ref
  18.0 20.3 %density.1.rho_ref = f32[2,2,2,128]{3,2,1,0:T(2,128)} custom-call(f32[4,4,4,8,128]{4,3,2,1,0:T(8,128)} %pad_maximum_fusion.src_ref, f32[2,2,2,128]{3,2,1,0:T(2,128)} %len_ref.1), custom_call_target="tpu_custom_call" | custom-call | tf_op jit(solution)/shard_map/density/pallas_call | solution.py:275
  38.3 1.5 %collective-permute-start.5 = (f32[2,2,2,1,128]{4,3,2,1,0:T(1,128)}, f32[2,2,2,1,128]{4,3,2,1,0:T(1,128)S(1)}, u32[]{:S(2)}, u32[]{:S(2)}) collective-permute-start(f32[2,2,2,1,128]{4,3,2,1,0:T(1,128)} %bitcast.9), channel_id=1, source_target_pairs={{0,16},{16,0},{1,17},{17,1},{2,18},{18,2},{3,19},{19,3},{4,20},{20... | collective-permute-start | bytes 12296 | tf_op jit(solution)/shard_map/ppermute | solution.py:30
  39.8 2.3 %collective-permute-done.5 = f32[2,2,2,1,128]{4,3,2,1,0:T(1,128)S(1)} collective-permute-done((f32[2,2,2,1,128]{4,3,2,1,0:T(1,128)}, f32[2,2,2,1,128]{4,3,2,1,0:T(1,128)S(1)}, u32[]{:S(2)}, u32[]{:S(2)}) %collective-permute-start.5) | collective-permute-done | bytes 4128 | tf_op jit(solution)/shard_map/ppermute | solution.py:30
  42.2 1.3 %collective-permute-start.6 = (f32[4,1,2,1,128]{4,3,2,1,0:T(1,128)S(1)}, f32[4,1,2,1,128]{4,3,2,1,0:T(1,128)S(1)}, u32[]{:S(2)}, u32[]{:S(2)}) collective-permute-start(f32[4,1,2,1,128]{4,3,2,1,0:T(1,128)S(1)} %get-tuple-element.21), channel_id=1, source_target_pairs={{0,4},{4,8},{8,12},{12,0},{1,5},{5,9},{9,13},{13,1},{2,6},{6,10},{... | collective-permute-start | bytes 12296 | tf_op jit(solution)/shard_map/ppermute | solution.py:34
  43.5 2.6 %collective-permute-start.7 = (f32[4,1,2,1,128]{4,3,2,1,0:T(1,128)S(1)}, f32[4,1,2,1,128]{4,3,2,1,0:T(1,128)S(1)}, u32[]{:S(2)}, u32[]{:S(2)}) collective-permute-start(f32[4,1,2,1,128]{4,3,2,1,0:T(1,128)S(1)} %get-tuple-element.22), channel_id=1, source_target_pairs={{0,12},{4,0},{8,4},{12,8},{1,13},{5,1},{9,5},{13,9},{2,14},{6,2},{... | collective-permute-start | bytes 12296 | tf_op jit(solution)/shard_map/ppermute | solution.py:37
  46.1 1.6 %collective-permute-done.6 = f32[4,1,2,1,128]{4,3,2,1,0:T(1,128)S(1)} collective-permute-done((f32[4,1,2,1,128]{4,3,2,1,0:T(1,128)S(1)}, f32[4,1,2,1,128]{4,3,2,1,0:T(1,128)S(1)}, u32[]{:S(2)}, u32[]{:S(2)}) %collective-permute-start.6) | collective-permute-done | bytes 4128 | tf_op jit(solution)/shard_map/ppermute | solution.py:34
  47.6 0.0 collective-permute-done.7
  47.7 0.1 collective-permute-start.8
  47.7 0.0 copy-start.1
  47.8 1.7 %collective-permute-start.9 = (f32[4,4,1,1,128]{4,3,2,1,0:T(1,128)S(1)}, f32[4,4,1,1,128]{4,3,2,1,0:T(1,128)S(1)}, u32[]{:S(2)}, u32[]{:S(2)}) collective-permute-start(f32[4,4,1,1,128]{4,3,2,1,0:T(1,128)S(1)} %get-tuple-element.14), channel_id=1, source_target_pairs={{0,3},{1,0},{2,1},{3,2},{4,7},{5,4},{6,5},{7,6},{8,11},{9,8},{10,9... | collective-permute-start | bytes 24584 | tf_op jit(solution)/shard_map/ppermute | solution.py:37
  49.5 13.0 %own.1.sum_ref = f32[2,2,2,8,128]{4,3,2,1,0:T(8,128)} custom-call(f32[4,4,4,8,128]{4,3,2,1,0:T(8,128)} %pad_maximum_fusion.src_ref, f32[2,2,2,128]{3,2,1,0:T(2,128)} %density.1.rho_ref), custom_call_target="tpu_custom_call" | custom-call | tf_op jit(solution)/shard_map/own/pallas_call | solution.py:289
  62.4 0.0 collective-permute-done.8
  62.5 0.0 collective-permute-done.9
  62.5 0.6 pad_maximum_fusion.3.rho_ref
  63.1 13.0 %their.1 = (f32[3,2,2,2,128]{4,3,2,1,0:T(2,128)}, f32[2,2,2,128]{3,2,1,0:T(2,128)}) custom-call(f32[4,4,4,8,128]{4,3,2,1,0:T(8,128)} %pad_maximum_fusion.src_ref, f32[4,4,4,1,128]{4,3,2,1,0:T(1,128)} %pad_maximum_fusion.3.rho_ref, f32[2,2,2,8,128]{4,3,2,1,0:T(8,128)} %own.1.sum_ref, s32[2,2,2,128]{3,2,1,0:T(2,128)} %act_ref.1), custom_call_target="tpu_custom_call" | custom-call | tf_op jit(solution)/shard_map/their/pallas_call | solution.py:295
  (16 shorter events, 0.1 us)
Async XLA Ops:
  0.6 0.7 copy-start.2
  1.4 0.7 copy-start.4
  1.4 0.7 copy-start.3
  2.1 4.9 %collective-permute-start = (f32[2,2,2,8,128]{4,3,2,1,0:T(8,128)S(1)}, f32[2,2,2,8,128]{4,3,2,1,0:T(8,128)S(1)}, u32[]{:S(2)}, u32[]{:S(2)}) collective-permute-start(f32[2,2,2,8,128]{4,3,2,1,0:T(8,128)S(1)} %stack.11), channel_id=1, source_target_pairs={{0,16},{16,0},{1,17},{17,1},{2,18},{18,2},{3,19},{19,3},{4,20},{20... | collective-permute-start | bytes 98312 | tf_op jit(solution)/shard_map/ppermute | solution.py:30
  7.1 6.2 %collective-permute-start.1 = (f32[4,1,2,8,128]{4,3,2,1,0:T(8,128)S(1)}, f32[4,1,2,8,128]{4,3,2,1,0:T(8,128)S(1)}, u32[]{:S(2)}, u32[]{:S(2)}) collective-permute-start(f32[4,1,2,8,128]{4,3,2,1,0:T(8,128)S(1)} %get-tuple-element.9), channel_id=1, source_target_pairs={{0,4},{4,8},{8,12},{12,0},{1,5},{5,9},{9,13},{13,1},{2,6},{6,10},{... | collective-permute-start | bytes 98312 | tf_op jit(solution)/shard_map/ppermute | solution.py:34
  9.2 4.3 %collective-permute-start.2 = (f32[4,1,2,8,128]{4,3,2,1,0:T(8,128)S(1)}, f32[4,1,2,8,128]{4,3,2,1,0:T(8,128)S(1)}, u32[]{:S(2)}, u32[]{:S(2)}) collective-permute-start(f32[4,1,2,8,128]{4,3,2,1,0:T(8,128)S(1)} %get-tuple-element.10), channel_id=1, source_target_pairs={{0,12},{4,0},{8,4},{12,8},{1,13},{5,1},{9,5},{13,9},{2,14},{6,2},{... | collective-permute-start | bytes 98312 | tf_op jit(solution)/shard_map/ppermute | solution.py:37
  13.5 3.7 %collective-permute-start.3 = (f32[4,4,1,8,128]{4,3,2,1,0:T(8,128)S(1)}, f32[4,4,1,8,128]{4,3,2,1,0:T(8,128)S(1)}, u32[]{:S(2)}, u32[]{:S(2)}) collective-permute-start(f32[4,4,1,8,128]{4,3,2,1,0:T(8,128)S(1)} %get-tuple-element.7), channel_id=1, source_target_pairs={{0,1},{1,2},{2,3},{3,0},{4,5},{5,6},{6,7},{7,4},{8,9},{9,10},{10,1... | collective-permute-start | bytes 196616 | tf_op jit(solution)/shard_map/ppermute | solution.py:34
  13.6 3.7 %collective-permute-start.4 = (f32[4,4,1,8,128]{4,3,2,1,0:T(8,128)S(1)}, f32[4,4,1,8,128]{4,3,2,1,0:T(8,128)S(1)}, u32[]{:S(2)}, u32[]{:S(2)}) collective-permute-start(f32[4,4,1,8,128]{4,3,2,1,0:T(8,128)S(1)} %get-tuple-element.8), channel_id=1, source_target_pairs={{0,3},{1,0},{2,1},{3,2},{4,7},{5,4},{6,5},{7,6},{8,11},{9,8},{10,9... | collective-permute-start | bytes 196616 | tf_op jit(solution)/shard_map/ppermute | solution.py:37
  38.3 3.8 %copy-start = (f32[2,2,2,128]{3,2,1,0:T(2,128)S(1)}, f32[2,2,2,128]{3,2,1,0:T(2,128)}, u32[]{:S(2)}) copy-start(f32[2,2,2,128]{3,2,1,0:T(2,128)} %density.1.rho_ref) | copy-start | bytes 12292
  38.3 3.8 %collective-permute-start.5 = (f32[2,2,2,1,128]{4,3,2,1,0:T(1,128)}, f32[2,2,2,1,128]{4,3,2,1,0:T(1,128)S(1)}, u32[]{:S(2)}, u32[]{:S(2)}) collective-permute-start(f32[2,2,2,1,128]{4,3,2,1,0:T(1,128)} %bitcast.9), channel_id=1, source_target_pairs={{0,16},{16,0},{1,17},{17,1},{2,18},{18,2},{3,19},{19,3},{4,20},{20... | collective-permute-start | bytes 12296 | tf_op jit(solution)/shard_map/ppermute | solution.py:30
  42.2 5.5 %collective-permute-start.6 = (f32[4,1,2,1,128]{4,3,2,1,0:T(1,128)S(1)}, f32[4,1,2,1,128]{4,3,2,1,0:T(1,128)S(1)}, u32[]{:S(2)}, u32[]{:S(2)}) collective-permute-start(f32[4,1,2,1,128]{4,3,2,1,0:T(1,128)S(1)} %get-tuple-element.21), channel_id=1, source_target_pairs={{0,4},{4,8},{8,12},{12,0},{1,5},{5,9},{9,13},{13,1},{2,6},{6,10},{... | collective-permute-start | bytes 12296 | tf_op jit(solution)/shard_map/ppermute | solution.py:34
  43.5 4.2 %collective-permute-start.7 = (f32[4,1,2,1,128]{4,3,2,1,0:T(1,128)S(1)}, f32[4,1,2,1,128]{4,3,2,1,0:T(1,128)S(1)}, u32[]{:S(2)}, u32[]{:S(2)}) collective-permute-start(f32[4,1,2,1,128]{4,3,2,1,0:T(1,128)S(1)} %get-tuple-element.22), channel_id=1, source_target_pairs={{0,12},{4,0},{8,4},{12,8},{1,13},{5,1},{9,5},{13,9},{2,14},{6,2},{... | collective-permute-start | bytes 12296 | tf_op jit(solution)/shard_map/ppermute | solution.py:37
  47.7 14.8 %collective-permute-start.8 = (f32[4,4,1,1,128]{4,3,2,1,0:T(1,128)S(1)}, f32[4,4,1,1,128]{4,3,2,1,0:T(1,128)S(1)}, u32[]{:S(2)}, u32[]{:S(2)}) collective-permute-start(f32[4,4,1,1,128]{4,3,2,1,0:T(1,128)S(1)} %get-tuple-element.13), channel_id=1, source_target_pairs={{0,1},{1,2},{2,3},{3,0},{4,5},{5,6},{6,7},{7,4},{8,9},{9,10},{10,1... | collective-permute-start | bytes 24584 | tf_op jit(solution)/shard_map/ppermute | solution.py:34
  47.7 14.7 %copy-start.1 = (f32[2,2,2,128]{3,2,1,0:T(2,128)S(1)}, f32[2,2,2,128]{3,2,1,0:T(2,128)}, u32[]{:S(2)}) copy-start(f32[2,2,2,128]{3,2,1,0:T(2,128)} %density.1.rho_ref) | copy-start | bytes 12292
  47.8 14.7 %collective-permute-start.9 = (f32[4,4,1,1,128]{4,3,2,1,0:T(1,128)S(1)}, f32[4,4,1,1,128]{4,3,2,1,0:T(1,128)S(1)}, u32[]{:S(2)}, u32[]{:S(2)}) collective-permute-start(f32[4,4,1,1,128]{4,3,2,1,0:T(1,128)S(1)} %get-tuple-element.14), channel_id=1, source_target_pairs={{0,3},{1,0},{2,1},{3,2},{4,7},{5,4},{6,5},{7,6},{8,11},{9,8},{10,9... | collective-permute-start | bytes 24584 | tf_op jit(solution)/shard_map/ppermute | solution.py:37
where the time goes:
time: 76.4 us; the launch traced here: 76.1 us
  Pallas kernels  46.3 us (61%)
  starting transfers between devices  16.2 us (21%)
  waiting for transfers between devices  9.93 us (13%)
  local copies, waits for them, and re-layouts  1.54 us (2%)
  other arithmetic  1.4 us (2%)
    pallas_call x1, Pallas kernels, body(): pl.pallas_call(functools.partial(density_kernel, sizes=sizes), out_shape=...  20.3 us
    pallas_call x1, Pallas kernels, body(): pl.pallas_call(functools.partial(their_kernel, sizes=sizes), out_shape=(j...  13 us
    pallas_call x1, Pallas kernels, body(): pl.pallas_call(functools.partial(own_kernel, sizes=sizes), out_shape=jax....  13 us
    ppermute x4, starting transfers between devices, halo(): lax.ppermute(lax.slice_in_dim(block, 0, 1, axis=dim), axis, ring(axis, -1))  8.14 us
    ppermute x4, waiting for transfers between devices, halo(): lax.ppermute(lax.slice_in_dim(block, size - 1, size, axis=dim), axis, rin...  5.45 us
    ppermute x2, starting transfers between devices, halo(): other = lax.ppermute(block, axis, ring(axis, 1))  4.52 us
    ppermute x2, waiting for transfers between devices, halo(): other = lax.ppermute(block, axis, ring(axis, 1))  4.22 us
    ppermute x4, starting transfers between devices, halo(): lax.ppermute(lax.slice_in_dim(block, size - 1, size, axis=dim), axis, rin...  3.56 us
  transfers between devices with their start and end apart: 10, of which 6 were waited for; matrix products, arithmetic and copies ran while one was open for 0% of the time, Pallas kernels for 17%

commit v1 on v0

v1 whole, which is shorter than its diff:
```python
import functools

import jax
import jax.numpy as jnp
from jax import lax
from jax.experimental import pallas as pl
from jax.experimental.pallas import tpu as pltpu
from jax.sharding import PartitionSpec as P

PASSES = 2

kernel_norm = 2.5464790894703255
eta_factor = 2.3
gamma_index = 5.0 / 3.0

ROWS = 32
TINY = 1e-12
VMEM_LIMIT = 24 * 1024 * 1024
AXES = ("gx", "gy", "gz")


def ring(axis, step):
    count = lax.axis_size(axis)
    return [(i, (i + step) % count) for i in range(count)]


def halo(block):
    for dim, axis in enumerate(AXES):
        size = block.shape[dim]
        if lax.axis_size(axis) == 2:
            other = lax.ppermute(block, axis, ring(axis, 1))
            low = lax.slice_in_dim(other, size - 1, size, axis=dim)
            high = lax.slice_in_dim(other, 0, 1, axis=dim)
        else:
            low = lax.ppermute(
                lax.slice_in_dim(block, size - 1, size, axis=dim), axis, ring(axis, 1)
            )
            high = lax.ppermute(lax.slice_in_dim(block, 0, 1, axis=dim), axis, ring(axis, -1))
        block = jnp.concatenate([low, block, high], axis=dim)
    return block


def cube_root(value):
    return jnp.exp(jnp.log(value) * (1.0 / 3.0))


def split3(value):
    high = value.astype(jnp.bfloat16).astype(jnp.float32)
    rest = value - high
    mid = rest.astype(jnp.bfloat16).astype(jnp.float32)
    return high, mid, rest - mid


def row_index():
    return lax.broadcasted_iota(jnp.int32, (8, 128), 0)


def place(fields, origin):
    row = row_index()
    shift = jnp.where(row == 0, origin[0], jnp.where(row == 1, origin[1], origin[2]))
    spot = jnp.where(row < 3, fields + shift, 0.0)
    return spot, jnp.sum(spot * spot, axis=0, keepdims=True)


def source_rows(spot, square, scale):
    row = row_index()
    value = jnp.where(row == 3, square, jnp.where(row == 4, 1.0, spot)) * scale
    high, mid, low = split3(value)
    return jnp.concatenate([high, mid, high, mid, low, high], axis=0)


def target_rows(spot, square, scale):
    row = row_index()
    value = jnp.where(row == 3, 1.0, jnp.where(row == 4, square, -2.0 * spot)) * scale
    high, mid, low = split3(value)
    return jnp.concatenate([high, high, mid, mid, high, low], axis=0)


def product(left, right):
    return jnp.dot(left, right, preferred_element_type=jnp.float32)


def product_nt(left, right):
    return lax.dot_general(
        left, right, (((1,), (1,)), ((), ())), preferred_element_type=jnp.float32
    )


def product_tn(left, right):
    return lax.dot_general(
        left, right, (((0,), (0,)), ((), ())), preferred_element_type=jnp.float32
    )


def tiled(rows, count):
    return jnp.concatenate([rows] * count, axis=0)


def origin_of(cell, sizes):
    return [c - 0.5 * n for c, n in zip(cell, sizes)]


def cells_of(sizes):
    return [(x, y, z) for x in range(sizes[0]) for y in range(sizes[1]) for z in range(sizes[2])]


def half_up(count):
    return jnp.floor((count + 1.0) * 0.5)


def sort_kernel(src_ref, side_ref, *, local):
    row = row_index()
    across = lax.broadcasted_iota(jnp.int32, (128, 128), 0)
    along = lax.broadcasted_iota(jnp.int32, (128, 128), 1)
    earlier = across < along

    def rank(key):
        left = jnp.broadcast_to(key, (8, 128)).T[:, 0:1]
        ahead = (left < key) | (earlier & (left == key))
        return jnp.sum(jnp.where(ahead, 1.0, 0.0), axis=0, keepdims=True)

    for index, cell in enumerate(cells_of(local)):
        fields = src_ref[cell]
        mass = fields[3:4]
        heavy = jnp.where(mass > jnp.sum(mass, axis=1, keepdims=True) * (1.0 / 128.0), 1.0, 0.0)
        light = 128.0 - jnp.sum(heavy, axis=1, keepdims=True)
        base = jnp.zeros((1, 128), jnp.float32)
        size = jnp.broadcast_to(light, (1, 128))
        group = jnp.zeros((1, 128), jnp.float32)
        bits = []
        for dim in range(3):
            place_in = rank(fields[dim : dim + 1] + 2.0 * group + 64.0 * heavy) - base
            first = half_up(size)
            bit = jnp.where(place_in >= first, 1.0, 0.0) * (1.0 - heavy)
            base = base + bit * first
            size = jnp.where(bit > 0.0, size - first, first)
            group = 2.0 * group + bit
            place_in = place_in - bit * first
            bits.append(bit)
        slot = jnp.where(heavy > 0.0, -1.0, 16.0 * group + place_in)
        side = jnp.where(row == 0, bits[0], jnp.where(row == 1, bits[1], bits[2]))
        side = jnp.where(row == 3, heavy, side)
        side_ref[index] = jnp.where(row == 4, slot, side)


def halves_of(source, count):
    reach = []
    for half in range(2 * count):
        cell = half // 2 + 1
        if source in ((cell - 1, cell) if half % 2 == 0 else (cell, cell + 1)):
            reach.append(half)
    return reach


def near_of(source, count):
    return [c for c in range(count) if abs(c + 1 - source) <= 1]


def runs_of(ranges, counts):
    xs, ys, zs = ranges
    return [
        (((x * counts[1] + y) * counts[2] + zs[0]) * 16, len(zs) * 16) for x in xs for y in ys
    ]


def main_kernel(
    src_ref,
    len_ref,
    side_ref,
    act_ref,
    rho_ref,
    push_ref,
    heat_ref,
    out_ref,
    dens_ref,
    root_ref,
    flat_ref,
    col_ref,
    size_ref,
    left_ref,
    feat_ref,
    oct_ref,
    rest_ref,
    far_ref,
    close_ref,
    own_ref,
    their_ref,
    sum_ref,
    count_ref,
    *,
    sizes,
):
    nx, ny, nz = sizes
    local = cx, cy, cz = nx - 2, ny - 2, nz - 2
    halves = (2 * cx, 2 * cy, 2 * cz)
    cells = cells_of(local)
    inner = len(cells) * 128
    row = row_index()
    across = lax.broadcasted_iota(jnp.int32, (128, 128), 0)
    along = lax.broadcasted_iota(jnp.int32, (128, 128), 1)
    before = jnp.where(across < along, 1.0, 0.0).astype(jnp.bfloat16)
    slot_of = across.astype(jnp.float32)
    first16 = lax.broadcasted_iota(jnp.int32, (16, 128), 0).astype(jnp.float32)

    for x, y, z in cells_of(sizes):
        fields = src_ref[x, y, z]
        spot, square = place(fields, origin_of((x, y, z), sizes))
        mass = fields[3:4]
        root = cube_root(mass)
        line = x * ny + y
        part = slice(z * 128, (z + 1) * 128)
        dens_ref[line, :, part] = source_rows(spot, square, root * root).astype(jnp.bfloat16)
        flat_ref[line, :, part] = source_rows(spot, square, 1.0).astype(jnp.bfloat16)
        root_ref[line, :, part] = jnp.broadcast_to(root, (8, 128))
        moving = jnp.sum(fields[4:7] * spot[0:3], axis=0, keepdims=True)
        basis = jnp.where(row < 3, spot, jnp.where(row == 3, 1.0, fields))
        basis = jnp.where(row == 7, moving, basis) * mass
        cols = jnp.concatenate(split3(basis), axis=0).T.astype(jnp.bfloat16)
        col_ref[line, z * 256 : z * 256 + 128, :] = cols
        col_ref[line, z * 256 + 128 : z * 256 + 256, :] = cols

    def spline(s, root):
        s = jnp.maximum(s, TINY)
        scaled = s * lax.rsqrt(s)
        t = root - scaled
        a = jnp.maximum(t, 0.0)
        b = jnp.maximum(t - scaled, 0.0)
        return a * a * a, b * b * b

    def dense_sums(left, x, y, z):
        count = left.shape[0]
        near = jnp.zeros((count, 128), jnp.float32)
        far = jnp.zeros((count, 128), jnp.float32)
        lanes = pl.ds(pl.multiple_of(z * 128, 128), 384)
        for dx in range(3):
            for dy in range(3):
                line = (x + dx) * ny + y + dy
                s = product(left, dens_ref[line, :, lanes])
                a, b = spline(s, tiled(root_ref[line, :, lanes], count // 8))
                for k in range(3):
                    far = far + a[:, k * 128 : (k + 1) * 128]
                    near = near + b[:, k * 128 : (k + 1) * 128]
        return 2.0 * far - near

    def first_pass(index, carry):
        x = index // (cy * cz)
        y = index // cz % cy
        z = index % cz
        fields = src_ref[x + 1, y + 1, z + 1]
        where = [v.astype(jnp.float32) + (1.0 - 0.5 * n) for v, n in zip((x, y, z), sizes)]
        spot, square = place(fields, where)
        inverse = 1.0 / len_ref[x, y, pl.ds(z, 1), :]
        left = target_rows(spot, square, inverse * inverse).T.astype(jnp.bfloat16)
        sums = [dense_sums(left[k : k + ROWS], x, y, z) for k in range(0, 128, ROWS)]
        total = jnp.sum(jnp.concatenate(sums, axis=0).T, axis=0, keepdims=True)
        density = kernel_norm * total * (inverse * inverse * inverse)
        length = eta_factor * cube_root(fields[3:4] / density)
        size_ref[index] = jnp.broadcast_to(length, (8, 128))
        return carry

    lax.fori_loop(0, cx * cy * cz, first_pass, 0)

    def cell_runs(cell):
        x, y, z = cell
        return [
            (((2 * x + bx) * halves[1] + 2 * y + by) * halves[2] + 2 * z) * 16
            for bx in range(2)
            for by in range(2)
        ]

    def scatter_rows(ref, index, cell, value):
        for k, start in enumerate(cell_runs(cell)):
            ref[start : start + 32, :] = value[k * 32 : (k + 1) * 32]

    def gather_rows(value_of, cell):
        return jnp.concatenate([value_of(start) for start in cell_runs(cell)], axis=0)

    def choose(index, fields, length):
        side = side_ref[index]
        reach = jnp.where(side > 0.0, length - fields, fields + length - 1.0)
        wide = jnp.where((row < 3) & (reach > 0.0), 1.0, 0.0)
        wide = jnp.where(row == 3, side, wide)
        wide = jnp.max(wide, axis=0, keepdims=True)
        order = product(jnp.broadcast_to(wide, (8, 128)).astype(jnp.bfloat16), before)[0:1]
        order = jnp.where(wide > 0.0, order, -1.0)
        count_ref[index] = jnp.sum(wide).astype(jnp.int32)
        slot = jnp.where(wide > 0.0, -1.0, side[4:5])
        oct_ref[index] = jnp.where(slot_of == slot, 1.0, 0.0).astype(jnp.bfloat16)
        rest_ref[index] = jnp.broadcast_to(order, (8, 128))
        return picked(index, 0)

    def picked(index, chunk):
        order = rest_ref[index][0:1]
        shift = jnp.float32(16.0) * chunk
        return jnp.where(first16 + shift == order, 1.0, 0.0)

    def set_rows(index, cell, fields, spot, square, length, weight):
        inverse = 1.0 / length
        rest = choose(index, fields, length).astype(jnp.bfloat16)
        left = target_rows(spot, square, inverse * inverse).astype(jnp.bfloat16)
        chosen = oct_ref[index]
        scatter_rows(left_ref, index, cell, product_nt(chosen, left).astype(jnp.bfloat16))
        part = slice(inner + index * 16, inner + index * 16 + 16)
        left_ref[part, :] = product_nt(rest, left).astype(jnp.bfloat16)
        if weight is not None:
            feat = jnp.concatenate(split3(weight), axis=0).astype(jnp.bfloat16)
            scatter_rows(feat_ref, index, cell, product_nt(chosen, feat).astype(jnp.bfloat16))
            feat_ref[part, :] = product_nt(rest, feat).astype(jnp.bfloat16)

    def source_runs(x, y, z):
        ranges = [halves_of(s, n) for s, n in zip((x, y, z), local)]
        runs = runs_of(ranges, halves)
        ranges = [near_of(s, n) for s, n in zip((x, y, z), local)]
        return runs + [(inner + start, size) for start, size in runs_of(ranges, local)]

    def rows_of(ref, runs):
        return jnp.concatenate([ref[start : start + size, :] for start, size in runs], axis=0)

    def add_rows(ref, runs, value):
        at = 0
        for start, size in runs:
            ref[start : start + size, :] += value[at : at + size]
            at += size

    def unsorted_column(index, octant, rest):
        total = jnp.sum(octant, axis=1, keepdims=True) * oct_ref[index].astype(jnp.float32)
        total = jnp.sum(total, axis=0, keepdims=True)
        rest = jnp.sum(rest, axis=1, keepdims=True) * picked(index, 0)
        return total + jnp.sum(rest, axis=0, keepdims=True)

    def extras(visit):
        def one_cell(index, carry):
            def one_chunk(chunk, carry):
                x = index // (cy * cz)
                y = index // cz % cy
                z = index % cz
                fields = src_ref[x + 1, y + 1, z + 1]
                where = [v.astype(jnp.float32) + (1.0 - 0.5 * n) for v, n in zip((x, y, z), sizes)]
                spot, square = place(fields, where)
                inverse = 1.0 / size_ref[index][0:1]
                rest = picked(index, chunk.astype(jnp.float32))
                left = target_rows(spot, square, inverse * inverse).astype(jnp.bfloat16)
                left = product_nt(rest.astype(jnp.bfloat16), left).astype(jnp.bfloat16)
                visit(index, (x, y, z), fields, spot, rest, left)
                return carry

            return lax.fori_loop(1, (count_ref[index] + 15) // 16, one_chunk, carry)

        lax.fori_loop(0, cx * cy * cz, one_cell, 0)

    def weight_of(fields, spot, strength):
        return jnp.where(row < 3, spot, jnp.where(row == 3, 1.0, 0.0)) * (fields[3:4] * strength)

    def extra_density(index, cell, fields, spot, rest, left):
        extra = jnp.sum(dense_sums(left, *cell), axis=1, keepdims=True) * rest
        sum_ref[index, 0:8, :] += jnp.sum(extra, axis=0, keepdims=True)

    def unsort(value, rest):
        pieces = split3(value)
        rest = rest.astype(jnp.bfloat16)
        total = product_tn(pieces[0].astype(jnp.bfloat16), rest)
        total += product_tn(pieces[1].astype(jnp.bfloat16), rest)
        return total + product_tn(pieces[2].astype(jnp.bfloat16), rest)

    def extra_force(index, cell, fields, spot, rest, left):
        x, y, z = cell
        feat = jnp.concatenate(split3(weight_of(fields, spot, size_ref[index][1:2])), axis=0)
        feat = product_nt(rest.astype(jnp.bfloat16), feat.astype(jnp.bfloat16))
        feat = feat.astype(jnp.bfloat16)
        total = jnp.zeros((16, 24), jnp.float32)
        for dx in range(3):
            for dy in range(3):
                line = (x + dx) * ny + y + dy
                lanes = pl.ds(pl.multiple_of(z * 128, 128), 384)
                high, low = profile(product(left, flat_ref[line, :, lanes]))
                for dz in range(3):
                    cols = col_ref[line, pl.ds(pl.multiple_of((z + dz) * 256, 256), 256), :]
                    part = slice(dz * 128, (dz + 1) * 128)
                    pair = jnp.concatenate([high[:, part], low[:, part]], axis=1)
                    total += product(pair, cols)
                their_ref[line, :, lanes] += product_tn(feat, high) + product_tn(feat, low)
        sum_ref[index] += unsort(total, rest)

    placed = []
    for index, cell in enumerate(cells):
        fields = src_ref[cell[0] + 1, cell[1] + 1, cell[2] + 1]
        origin = origin_of([c + 1 for c in cell], sizes)
        placed.append((fields, origin))
        spot, square = place(fields, origin)
        set_rows(index, cell, fields, spot, square, size_ref[index][0:1], None)

    far_ref[...] = jnp.zeros_like(far_ref)
    close_ref[...] = jnp.zeros_like(close_ref)
    for x, y, z in cells_of(sizes):
        runs = source_runs(x, y, z)
        line = x * ny + y
        part = slice(z * 128, (z + 1) * 128)
        left = rows_of(left_ref, runs)
        s = product(left, dens_ref[line, :, part])
        a, b = spline(s, tiled(root_ref[line, :, part], left.shape[0] // 8))
        add_rows(far_ref, runs, a)
        add_rows(close_ref, runs, b)

    for index, cell in enumerate(cells):
        part = slice(inner + index * 16, inner + index * 16 + 16)
        octant = gather_rows(
            lambda start: 2.0 * far_ref[start : start + 32, :] - close_ref[start : start + 32, :],
            cell,
        )
        total = unsorted_column(index, octant, 2.0 * far_ref[part, :] - close_ref[part, :])
        sum_ref[index, 0:8, :] = jnp.broadcast_to(total, (8, 128))
    extras(extra_density)
    for index, cell in enumerate(cells):
        x, y, z = cell
        fields, origin = placed[index]
        spot, square = place(fields, origin)
        inverse = 1.0 / size_ref[index][0:1]
        density = kernel_norm * sum_ref[index, 0:1, :] * (inverse * inverse * inverse)
        rho_ref[x, y, z : z + 1, :] = density
        length = eta_factor * cube_root(fields[3:4] / density)
        inv2, strength = smooth(fields, density)
        size_ref[index] = jnp.where(row == 0, length, strength)
        set_rows(index, cell, fields, spot, square, length, weight_of(fields, spot, strength))

    own_ref[...] = jnp.zeros_like(own_ref)

    def slopes(x, y, z):
        runs = source_runs(x, y, z)
        line = x * ny + y
        part = slice(z * 128, (z + 1) * 128)
        high, low = profile(product(rows_of(left_ref, runs), flat_ref[line, :, part]))
        return line, z, runs, high, low

    def sums(line, z, runs, high, low):
        part = slice(z * 128, (z + 1) * 128)
        cols = col_ref[line, z * 256 : (z + 1) * 256, :]
        add_rows(own_ref, runs, product(jnp.concatenate([high, low], axis=1), cols))
        feat = rows_of(feat_ref, runs)
        their_ref[line, :, part] = product_tn(feat, high) + product_tn(feat, low)

    waiting = None
    for source in cells_of(sizes):
        ready = slopes(*source)
        if waiting is not None:
            sums(*waiting)
        waiting = ready
    sums(*waiting)

    for index, cell in enumerate(cells):
        octant = gather_rows(lambda start: own_ref[start : start + 32, :], cell)
        part = slice(inner + index * 16, inner + index * 16 + 16)
        own = unsort(octant, oct_ref[index]) + unsort(own_ref[part, :], picked(index, 0))
        sum_ref[index] = own
    extras(extra_force)
    for index, cell in enumerate(cells):
        x, y, z = cell
        fields, origin = placed[index]
        spot, square = place(fields, origin)
        own = sum_ref[index]
        own = (own[0:8] + own[8:16] + own[16:24]) * size_ref[index][1:2]
        active = act_ref[x, y, z : z + 1, :].astype(jnp.float32)
        spot = spot[0:3]
        push = spot * own[3:4] - own[0:3]
        heat = fields[4:7] * push - spot * own[4:7]
        heat = jnp.sum(heat, axis=0, keepdims=True) + own[7:8]
        push_ref[x, y, z] = jnp.concatenate([push, active], axis=0)
        heat_ref[x, y, z : z + 1, :] = active * heat

    for x, y, z in cells_of(sizes):
        spot, square = place(src_ref[x, y, z], origin_of((x, y, z), sizes))
        their = their_ref[x * ny + y, :, z * 128 : (z + 1) * 128]
        their = their[0:8] + their[8:16] + their[16:24]
        out_ref[x, y, z] = (spot * their[3:4] - their)[0:4]


def profile(s):
    s = jnp.maximum(s, TINY)
    rs = lax.rsqrt(s)
    q = s * rs
    t = 1.0 - q
    a = jnp.maximum(t, 0.0)
    b = jnp.maximum(t - q, 0.0)
    g = jnp.minimum(a, q) * (a + b) * rs
    high = g.astype(jnp.bfloat16)
    return high, (g - high.astype(jnp.float32)).astype(jnp.bfloat16)


def smooth(fields, density):
    inverse = 1.0 / (eta_factor * cube_root(fields[3:4] / density))
    inv2 = inverse * inverse
    press = (gamma_index - 1.0) * fields[7:8] / density
    return inv2, press * (-6.0 * kernel_norm) * inv2 * inv2 * inverse


def take(block, dim, start, stop):
    return lax.slice_in_dim(block, start, stop, axis=dim)


def fold(block):
    for dim in (2, 1, 0):
        axis = AXES[dim]
        last = block.shape[dim] - 1
        low, high = take(block, dim, 0, 1), take(block, dim, last, last + 1)
        if lax.axis_size(axis) == 2:
            both = lax.ppermute(jnp.concatenate([high, low], axis=dim), axis, ring(axis, 1))
            to_first, to_last = take(both, dim, 0, 1), take(both, dim, 1, 2)
        else:
            to_last = lax.ppermute(low, axis, ring(axis, -1))
            to_first = lax.ppermute(high, axis, ring(axis, 1))
        block = take(block, dim, 1, last)
        count = last - 1
        if count == 1:
            block = block + to_first + to_last
        else:
            block = jnp.concatenate(
                [
                    take(block, dim, 0, 1) + to_first,
                    take(block, dim, 1, count - 1),
                    take(block, dim, count - 1, count) + to_last,
                ],
                axis=dim,
            )
    return block


def body(offsets, masses, smoothing, velocity, energy, active):
    local = masses.shape[:3]
    sizes = tuple(n + 2 for n in local)
    nx, ny, nz = sizes
    f32 = jnp.float32
    bf16 = jnp.bfloat16
    ncell = local[0] * local[1] * local[2]
    static = jnp.stack(
        [offsets[0], offsets[1], offsets[2], masses, velocity[0], velocity[1], velocity[2], energy],
        axis=3,
    )
    side = pl.pallas_call(
        functools.partial(sort_kernel, local=local),
        out_shape=jax.ShapeDtypeStruct((ncell, 8, 128), f32),
        compiler_params=pltpu.CompilerParams(vmem_limit_bytes=VMEM_LIMIT),
        name="sort",
    )(static)
    padded = halo(static)
    lines = nx * ny
    rows = ncell * 144
    density, push, heat, spread = pl.pallas_call(
        functools.partial(main_kernel, sizes=sizes),
        out_shape=(
            jax.ShapeDtypeStruct(masses.shape, f32),
            jax.ShapeDtypeStruct(local + (4, 128), f32),
            jax.ShapeDtypeStruct(masses.shape, f32),
            jax.ShapeDtypeStruct(sizes + (4, 128), f32),
        ),
        scratch_shapes=[
            pltpu.VMEM((lines, 48, nz * 128), bf16),
            pltpu.VMEM((lines, 8, nz * 128), f32),
            pltpu.VMEM((lines, 48, nz * 128), bf16),
            pltpu.VMEM((lines, nz * 256, 24), bf16),
            pltpu.VMEM((ncell, 8, 128), f32),
            pltpu.VMEM((rows, 48), bf16),
            pltpu.VMEM((rows, 24), bf16),
            pltpu.VMEM((ncell, 128, 128), bf16),
            pltpu.VMEM((ncell, 8, 128), f32),
            pltpu.VMEM((rows, 128), f32),
            pltpu.VMEM((rows, 128), f32),
            pltpu.VMEM((rows, 24), f32),
            pltpu.VMEM((lines, 24, nz * 128), f32),
            pltpu.VMEM((ncell, 24, 128), f32),
            pltpu.SMEM((ncell,), jnp.int32),
        ],
        compiler_params=pltpu.CompilerParams(vmem_limit_bytes=VMEM_LIMIT),
        name="main",
    )(padded, smoothing, side, active)
    total = -(push[..., 0:3, :] + fold(spread)[..., 0:3, :]) * push[..., 3:4, :]
    return (density, jnp.moveaxis(total, 3, 0), heat)


def solution(mesh):
    vector = P(None, "gx", "gy", "gz", None)
    scalar = P("gx", "gy", "gz", None)
    return jax.shard_map(
        body,
        mesh=mesh,
        in_specs=(vector, scalar, scalar, vector, scalar, scalar),
        out_specs=(scalar, vector, scalar),
        check_vma=False,
    )
```

time: 76.4 us -> 88 us (1.15); the launches traced: 76.1 us -> 89 us
  starting transfers between devices: 16.2 us -> 44.8 us
  Pallas kernels: 46.3 us -> 25.9 us
  waiting for transfers between devices: 9.93 us -> 14.7 us
  other arithmetic: 1.4 us -> 0.13 us
  local copies, waits for them, and re-layouts: 1.54 us -> 2.77 us
    ppermute x0 -> x5, starting transfers between devices: none -> 35.7 us  [the longest x1 18.9 us: fold(): lax.ppermute(jnp.concatenate([high, low], axis=dim), axis, ring(axis, 1))]
    pallas_call x3 -> x2, Pallas kernels: 46.3 us -> 25.9 us  [the longest x1 23 us: body(): pl.pallas_call(functools.partial(main_kernel, sizes=sizes), out_shape=(ja...]
    ppermute x0 -> x5, waiting for transfers between devices: none -> 10.6 us  [the longest x2 6.38 us: fold(): to_last = lax.ppermute(low, axis, ring(axis, -1))]
    ppermute x4 -> x2, starting transfers between devices: 8.14 us -> 3.82 us  [halo(): lax.ppermute(lax.slice_in_dim(block, 0, 1, axis=dim), axis, ring(axis, -1))]
    ppermute x4 -> x2, waiting for transfers between devices: 5.45 us -> 1.93 us  [halo(): lax.ppermute(lax.slice_in_dim(block, size - 1, size, axis=dim), axis, rin...]
    ppermute x2 -> x1, waiting for transfers between devices: 4.22 us -> 1.89 us  [halo(): other = lax.ppermute(block, axis, ring(axis, 1))]
    ppermute x2 -> x1, starting transfers between devices: 4.52 us -> 3.03 us  [halo(): other = lax.ppermute(block, axis, ring(axis, 1))]
    concatenate x6 -> x3, other arithmetic: 1.4 us -> 0.04 us  [halo(): block = jnp.concatenate([low, block, high], axis=dim)]
  transfers between devices with their start and end apart: 10 -> 10, of which waited for: 6 -> 7; matrix products, arithmetic and copies ran while one was open for 0% -> 0% of each run, Pallas kernels for 17% -> 3%
where the time goes in v1:
time: 88 us; the launch traced here: 89 us
  starting transfers between devices  44.8 us (51%)
  Pallas kernels  25.9 us (29%)
  waiting for transfers between devices  14.7 us (17%)
  local copies, waits for them, and re-layouts  2.77 us (3%)
    pallas_call x1, Pallas kernels, body(): pl.pallas_call(functools.partial(main_kernel, sizes=sizes), out_shape=(ja...  23 us
    ppermute x1, starting transfers between devices, fold(): lax.ppermute(jnp.concatenate([high, low], axis=dim), axis, ring(axis, 1))  18.9 us
    ppermute x2, starting transfers between devices, fold(): to_last = lax.ppermute(low, axis, ring(axis, -1))  9.37 us
    ppermute x2, starting transfers between devices, fold(): to_first = lax.ppermute(high, axis, ring(axis, 1))  7.46 us
    ppermute x2, waiting for transfers between devices, fold(): to_last = lax.ppermute(low, axis, ring(axis, -1))  6.38 us
    ppermute x2, starting transfers between devices, halo(): lax.ppermute(lax.slice_in_dim(block, 0, 1, axis=dim), axis, ring(axis, -1))  3.82 us
    ppermute x1, starting transfers between devices, halo(): other = lax.ppermute(block, axis, ring(axis, 1))  3.03 us
    pallas_call x1, Pallas kernels, body(): pl.pallas_call(functools.partial(sort_kernel, local=local), out_shape=jax...  2.95 us
  transfers between devices with their start and end apart: 10, of which 7 were waited for; matrix products, arithmetic and copies ran while one was open for 0% of the time, Pallas kernels for 3%

profile of v1, /device:TPU:0, one launch (start us, length us, event | category | flops | bytes accessed | tf_op | source)
XLA Modules:
  0.0 89.0 jit_solution(5487987051237260683)
XLA Ops:
  0.6 0.7 fusion.17
  1.4 0.0 copy-start.3
  1.4 0.7 copy-done.4
  2.1 0.0 copy-done.3
  2.1 0.1 stack.11.src_ref
  2.1 3.0 %collective-permute-start = (f32[2,2,2,8,128]{4,3,2,1,0:T(8,128)S(1)}, f32[2,2,2,8,128]{4,3,2,1,0:T(8,128)S(1)}, u32[]{:S(2)}, u32[]{:S(2)}) collective-permute-start(f32[2,2,2,8,128]{4,3,2,1,0:T(8,128)S(1)} %stack.11.src_ref), channel_id=1, source_target_pairs={{0,16},{16,0},{1,17},{17,1},{2,18},{18,2},{3,19},{19,3},{4,20},{20... | collective-permute-start | bytes 98312 | tf_op jit(solution)/shard_map/ppermute | solution.py:31
  5.2 1.9 %collective-permute-done = f32[2,2,2,8,128]{4,3,2,1,0:T(8,128)S(1)} collective-permute-done((f32[2,2,2,8,128]{4,3,2,1,0:T(8,128)S(1)}, f32[2,2,2,8,128]{4,3,2,1,0:T(8,128)S(1)}, u32[]{:S(2)}, u32[]{:S(2)}) %collective-permute-start) | collective-permute-done | bytes 32800 | tf_op jit(solution)/shard_map/ppermute | solution.py:31
  7.1 2.2 %collective-permute-start.1 = (f32[4,1,2,8,128]{4,3,2,1,0:T(8,128)S(1)}, f32[4,1,2,8,128]{4,3,2,1,0:T(8,128)S(1)}, u32[]{:S(2)}, u32[]{:S(2)}) collective-permute-start(f32[4,1,2,8,128]{4,3,2,1,0:T(8,128)S(1)} %get-tuple-element.22), channel_id=1, source_target_pairs={{0,4},{4,8},{8,12},{12,0},{1,5},{5,9},{9,13},{13,1},{2,6},{6,10},{... | collective-permute-start | bytes 98312 | tf_op jit(solution)/shard_map/ppermute | solution.py:35
  9.2 2.1 %collective-permute-start.2 = (f32[4,1,2,8,128]{4,3,2,1,0:T(8,128)S(1)}, f32[4,1,2,8,128]{4,3,2,1,0:T(8,128)S(1)}, u32[]{:S(2)}, u32[]{:S(2)}) collective-permute-start(f32[4,1,2,8,128]{4,3,2,1,0:T(8,128)S(1)} %get-tuple-element.23), channel_id=1, source_target_pairs={{0,12},{4,0},{8,4},{12,8},{1,13},{5,1},{9,5},{13,9},{2,14},{6,2},{... | collective-permute-start | bytes 98312 | tf_op jit(solution)/shard_map/ppermute | solution.py:38
  11.3 1.9 %collective-permute-done.1 = f32[4,1,2,8,128]{4,3,2,1,0:T(8,128)S(1)} collective-permute-done((f32[4,1,2,8,128]{4,3,2,1,0:T(8,128)S(1)}, f32[4,1,2,8,128]{4,3,2,1,0:T(8,128)S(1)}, u32[]{:S(2)}, u32[]{:S(2)}) %collective-permute-start.1) | collective-permute-done | bytes 32800 | tf_op jit(solution)/shard_map/ppermute | solution.py:35
  13.3 0.2 collective-permute-done.2
  13.5 0.1 collective-permute-start.3
  13.6 1.7 %collective-permute-start.4 = (f32[4,4,1,8,128]{4,3,2,1,0:T(8,128)S(1)}, f32[4,4,1,8,128]{4,3,2,1,0:T(8,128)S(1)}, u32[]{:S(2)}, u32[]{:S(2)}) collective-permute-start(f32[4,4,1,8,128]{4,3,2,1,0:T(8,128)S(1)} %get-tuple-element.17), channel_id=1, source_target_pairs={{0,3},{1,0},{2,1},{3,2},{4,7},{5,4},{6,5},{7,6},{8,11},{9,8},{10,9... | collective-permute-start | bytes 196616 | tf_op jit(solution)/shard_map/ppermute | solution.py:38
  15.3 2.9 %sort.1.side_ref = f32[8,8,128]{2,1,0:T(8,128)S(1)} custom-call(f32[2,2,2,8,128]{4,3,2,1,0:T(8,128)S(1)} %stack.11.src_ref), custom_call_target="tpu_custom_call" | custom-call | tf_op jit(solution)/shard_map/sort/pallas_call | solution.py:537
  18.3 0.0 copy-start
  18.3 0.0 copy-start.1
  18.3 0.0 collective-permute-done.3
  18.3 0.0 collective-permute-done.4
  18.4 0.6 copy-done
  19.0 0.0 copy-done.1
  19.0 23.0 %main.1 = (f32[2,2,2,128]{3,2,1,0:T(2,128)}, f32[2,2,2,4,128]{4,3,2,1,0:T(4,128)S(1)}, f32[2,2,2,128]{3,2,1,0:T(2,128)}, f32[4,4,4,4,128]{4,3,2,1,0:T(4,128)S(1)}) custom-call(f32[4,4,4,8,128]{4,3,2,1,0:T(8,128)S(1)} %pad_maximum_fusion.src_ref, f32[2,2,2,128]{3,2,1,0:T(2,128)S(1)} %copy-done, f32[8,8,128]{2,1,0:T(8,128)S(1)} %sort.1.side_ref, ...), custom_call_target="tpu_custom_call" | custom-call | tf_op jit(solution)/shard_map/main/pallas_call | solution.py:546
  42.0 0.1 collective-permute-start.6
  42.1 6.4 %collective-permute-done.6 = f32[4,4,1,4,128]{4,3,2,1,0:T(4,128)S(1)} collective-permute-done((f32[4,4,1,4,128]{4,3,2,1,0:T(4,128)S(1)}, f32[4,4,1,4,128]{4,3,2,1,0:T(4,128)S(1)}, u32[]{:S(2)}, u32[]{:S(2)}) %collective-permute-start.6) | collective-permute-done | bytes 32800 | tf_op jit(solution)/shard_map/ppermute | solution.py:508
  48.5 2.7 %collective-permute-start.5 = (f32[4,4,1,4,128]{4,3,2,1,0:T(4,128)S(1)}, f32[4,4,1,4,128]{4,3,2,1,0:T(4,128)S(1)}, u32[]{:S(2)}, u32[]{:S(2)}) collective-permute-start(f32[4,4,1,4,128]{4,3,2,1,0:T(4,128)S(1)} %get-tuple-element.15), channel_id=1, source_target_pairs={{0,1},{1,2},{2,3},{3,0},{4,5},{5,6},{6,7},{7,4},{8,9},{9,10},{10,1... | collective-permute-start | bytes 98312 | tf_op jit(solution)/shard_map/ppermute | solution.py:509
  51.2 0.9 collective-permute-done.5
  52.1 4.8 %collective-permute-start.7 = (f32[4,1,2,4,128]{4,3,2,1,0:T(4,128)S(1)}, f32[4,1,2,4,128]{4,3,2,1,0:T(4,128)S(1)}, u32[]{:S(2)}, u32[]{:S(2)}) collective-permute-start(f32[4,1,2,4,128]{4,3,2,1,0:T(4,128)S(1)} %get-tuple-element.21), channel_id=1, source_target_pairs={{0,4},{4,8},{8,12},{12,0},{1,5},{5,9},{9,13},{13,1},{2,6},{6,10},{... | collective-permute-start | bytes 49160 | tf_op jit(solution)/shard_map/ppermute | solution.py:509
  56.8 9.3 %collective-permute-start.8 = (f32[4,1,2,4,128]{4,3,2,1,0:T(4,128)S(1)}, f32[4,1,2,4,128]{4,3,2,1,0:T(4,128)S(1)}, u32[]{:S(2)}, u32[]{:S(2)}) collective-permute-start(f32[4,1,2,4,128]{4,3,2,1,0:T(4,128)S(1)} %get-tuple-element.20), channel_id=1, source_target_pairs={{0,12},{4,0},{8,4},{12,8},{1,13},{5,1},{9,5},{13,9},{2,14},{6,2},{... | collective-permute-start | bytes 49160 | tf_op jit(solution)/shard_map/ppermute | solution.py:508
  66.1 1.7 %collective-permute-done.7 = f32[4,1,2,4,128]{4,3,2,1,0:T(4,128)S(1)} collective-permute-done((f32[4,1,2,4,128]{4,3,2,1,0:T(4,128)S(1)}, f32[4,1,2,4,128]{4,3,2,1,0:T(4,128)S(1)}, u32[]{:S(2)}, u32[]{:S(2)}) %collective-permute-start.7) | collective-permute-done | bytes 16416 | tf_op jit(solution)/shard_map/ppermute | solution.py:509
  67.7 0.0 collective-permute-done.8
  67.8 18.9 %collective-permute-start.9 = (f32[2,2,2,4,128]{4,3,2,1,0:T(4,128)S(1)}, f32[2,2,2,4,128]{4,3,2,1,0:T(4,128)S(1)}, u32[]{:S(2)}, u32[]{:S(2)}) collective-permute-start(f32[2,2,2,4,128]{4,3,2,1,0:T(4,128)S(1)} %pad_maximum_fusion.5), channel_id=1, source_target_pairs={{0,16},{16,0},{1,17},{17,1},{2,18},{18,2},{3,19},{19,3},{4,20},{20... | collective-permute-start | bytes 49160 | tf_op jit(solution)/shard_map/ppermute | solution.py:505
  86.7 1.7 %collective-permute-done.9 = f32[2,2,2,4,128]{4,3,2,1,0:T(4,128)S(1)} collective-permute-done((f32[2,2,2,4,128]{4,3,2,1,0:T(4,128)S(1)}, f32[2,2,2,4,128]{4,3,2,1,0:T(4,128)S(1)}, u32[]{:S(2)}, u32[]{:S(2)}) %collective-permute-start.9) | collective-permute-done | bytes 16416 | tf_op jit(solution)/shard_map/ppermute | solution.py:505
  88.4 0.6 copy.9
  (20 shorter events, 0.2 us)
Async XLA Ops:
  0.6 0.7 copy-start.2
  1.4 0.7 copy-start.4
  1.4 0.7 copy-start.3
  2.1 4.9 %collective-permute-start = (f32[2,2,2,8,128]{4,3,2,1,0:T(8,128)S(1)}, f32[2,2,2,8,128]{4,3,2,1,0:T(8,128)S(1)}, u32[]{:S(2)}, u32[]{:S(2)}) collective-permute-start(f32[2,2,2,8,128]{4,3,2,1,0:T(8,128)S(1)} %stack.11.src_ref), channel_id=1, source_target_pairs={{0,16},{16,0},{1,17},{17,1},{2,18},{18,2},{3,19},{19,3},{4,20},{20... | collective-permute-start | bytes 98312 | tf_op jit(solution)/shard_map/ppermute | solution.py:31
  7.1 6.2 %collective-permute-start.1 = (f32[4,1,2,8,128]{4,3,2,1,0:T(8,128)S(1)}, f32[4,1,2,8,128]{4,3,2,1,0:T(8,128)S(1)}, u32[]{:S(2)}, u32[]{:S(2)}) collective-permute-start(f32[4,1,2,8,128]{4,3,2,1,0:T(8,128)S(1)} %get-tuple-element.22), channel_id=1, source_target_pairs={{0,4},{4,8},{8,12},{12,0},{1,5},{5,9},{9,13},{13,1},{2,6},{6,10},{... | collective-permute-start | bytes 98312 | tf_op jit(solution)/shard_map/ppermute | solution.py:35
  9.2 4.3 %collective-permute-start.2 = (f32[4,1,2,8,128]{4,3,2,1,0:T(8,128)S(1)}, f32[4,1,2,8,128]{4,3,2,1,0:T(8,128)S(1)}, u32[]{:S(2)}, u32[]{:S(2)}) collective-permute-start(f32[4,1,2,8,128]{4,3,2,1,0:T(8,128)S(1)} %get-tuple-element.23), channel_id=1, source_target_pairs={{0,12},{4,0},{8,4},{12,8},{1,13},{5,1},{9,5},{13,9},{2,14},{6,2},{... | collective-permute-start | bytes 98312 | tf_op jit(solution)/shard_map/ppermute | solution.py:38
  13.5 4.8 %collective-permute-start.3 = (f32[4,4,1,8,128]{4,3,2,1,0:T(8,128)S(1)}, f32[4,4,1,8,128]{4,3,2,1,0:T(8,128)S(1)}, u32[]{:S(2)}, u32[]{:S(2)}) collective-permute-start(f32[4,4,1,8,128]{4,3,2,1,0:T(8,128)S(1)} %get-tuple-element.16), channel_id=1, source_target_pairs={{0,1},{1,2},{2,3},{3,0},{4,5},{5,6},{6,7},{7,4},{8,9},{9,10},{10,1... | collective-permute-start | bytes 196616 | tf_op jit(solution)/shard_map/ppermute | solution.py:35
  13.6 4.7 %collective-permute-start.4 = (f32[4,4,1,8,128]{4,3,2,1,0:T(8,128)S(1)}, f32[4,4,1,8,128]{4,3,2,1,0:T(8,128)S(1)}, u32[]{:S(2)}, u32[]{:S(2)}) collective-permute-start(f32[4,4,1,8,128]{4,3,2,1,0:T(8,128)S(1)} %get-tuple-element.17), channel_id=1, source_target_pairs={{0,3},{1,0},{2,1},{3,2},{4,7},{5,4},{6,5},{7,6},{8,11},{9,8},{10,9... | collective-permute-start | bytes 196616 | tf_op jit(solution)/shard_map/ppermute | solution.py:38
  18.3 0.7 copy-start
  18.3 0.7 copy-start.1
  42.0 6.5 %collective-permute-start.6 = (f32[4,4,1,4,128]{4,3,2,1,0:T(4,128)S(1)}, f32[4,4,1,4,128]{4,3,2,1,0:T(4,128)S(1)}, u32[]{:S(2)}, u32[]{:S(2)}) collective-permute-start(f32[4,4,1,4,128]{4,3,2,1,0:T(4,128)S(1)} %slice.112), channel_id=1, source_target_pairs={{0,3},{1,0},{2,1},{3,2},{4,7},{5,4},{6,5},{7,6},{8,11},{9,8},{10,9... | collective-permute-start | bytes 98312 | tf_op jit(solution)/shard_map/ppermute | solution.py:508
  48.5 3.5 %collective-permute-start.5 = (f32[4,4,1,4,128]{4,3,2,1,0:T(4,128)S(1)}, f32[4,4,1,4,128]{4,3,2,1,0:T(4,128)S(1)}, u32[]{:S(2)}, u32[]{:S(2)}) collective-permute-start(f32[4,4,1,4,128]{4,3,2,1,0:T(4,128)S(1)} %get-tuple-element.15), channel_id=1, source_target_pairs={{0,1},{1,2},{2,3},{3,0},{4,5},{5,6},{6,7},{7,4},{8,9},{9,10},{10,1... | collective-permute-start | bytes 98312 | tf_op jit(solution)/shard_map/ppermute | solution.py:509
  52.1 15.7 %collective-permute-start.7 = (f32[4,1,2,4,128]{4,3,2,1,0:T(4,128)S(1)}, f32[4,1,2,4,128]{4,3,2,1,0:T(4,128)S(1)}, u32[]{:S(2)}, u32[]{:S(2)}) collective-permute-start(f32[4,1,2,4,128]{4,3,2,1,0:T(4,128)S(1)} %get-tuple-element.21), channel_id=1, source_target_pairs={{0,4},{4,8},{8,12},{12,0},{1,5},{5,9},{9,13},{13,1},{2,6},{6,10},{... | collective-permute-start | bytes 49160 | tf_op jit(solution)/shard_map/ppermute | solution.py:509
  56.8 10.9 %collective-permute-start.8 = (f32[4,1,2,4,128]{4,3,2,1,0:T(4,128)S(1)}, f32[4,1,2,4,128]{4,3,2,1,0:T(4,128)S(1)}, u32[]{:S(2)}, u32[]{:S(2)}) collective-permute-start(f32[4,1,2,4,128]{4,3,2,1,0:T(4,128)S(1)} %get-tuple-element.20), channel_id=1, source_target_pairs={{0,12},{4,0},{8,4},{12,8},{1,13},{5,1},{9,5},{13,9},{2,14},{6,2},{... | collective-permute-start | bytes 49160 | tf_op jit(solution)/shard_map/ppermute | solution.py:508
  67.8 20.6 %collective-permute-start.9 = (f32[2,2,2,4,128]{4,3,2,1,0:T(4,128)S(1)}, f32[2,2,2,4,128]{4,3,2,1,0:T(4,128)S(1)}, u32[]{:S(2)}, u32[]{:S(2)}) collective-permute-start(f32[2,2,2,4,128]{4,3,2,1,0:T(4,128)S(1)} %pad_maximum_fusion.5), channel_id=1, source_target_pairs={{0,16},{16,0},{1,17},{17,1},{2,18},{18,2},{3,19},{19,3},{4,20},{20... | collective-permute-start | bytes 49160 | tf_op jit(solution)/shard_map/ppermute | solution.py:505

commit v2 on v1

--- a/solution.py
+++ b/solution.py
@@ -7,7 +7,6 @@
 from jax.experimental.pallas import tpu as pltpu
 from jax.sharding import PartitionSpec as P
 
-PASSES = 2
 
 kernel_norm = 2.5464790894703255
 eta_factor = 2.3
@@ -15,6 +14,7 @@
 
 ROWS = 32
 TINY = 1e-12
+WIDE = 32
 VMEM_LIMIT = 24 * 1024 * 1024
 AXES = ("gx", "gy", "gz")
 
@@ -24,18 +24,22 @@
     return [(i, (i + step) % count) for i in range(count)]
 
 
-def halo(block):
-    for dim, axis in enumerate(AXES):
+def move(block, axis, step):
+    return lax.ppermute(block, axis, ring(axis, step))
+
+
+def halo(block, dims):
+    for dim in dims:
+        axis = AXES[dim]
         size = block.shape[dim]
         if lax.axis_size(axis) == 2:
-            other = lax.ppermute(block, axis, ring(axis, 1))
+            other = move(block, axis, 1)
             low = lax.slice_in_dim(other, size - 1, size, axis=dim)
             high = lax.slice_in_dim(other, 0, 1, axis=dim)
         else:
-            low = lax.ppermute(
-                lax.slice_in_dim(block, size - 1, size, axis=dim), axis, ring(axis, 1)
-            )
-            high = lax.ppermute(lax.slice_in_dim(block, 0, 1, axis=dim), axis, ring(axis, -1))
+            low = lax.slice_in_dim(block, size - 1, size, axis=dim)
+            low = move(low, axis, 1)
+            high = move(lax.slice_in_dim(block, 0, 1, axis=dim), axis, -1)
         block = jnp.concatenate([low, block, high], axis=dim)
     return block
 
@@ -104,11 +108,91 @@
     return [(x, y, z) for x in range(sizes[0]) for y in range(sizes[1]) for z in range(sizes[2])]
 
 
+def spline(s, root):
+    s = jnp.maximum(s, TINY)
+    scaled = s * lax.rsqrt(s)
+    t = root - scaled
+    a = jnp.maximum(t, 0.0)
+    b = jnp.maximum(t - scaled, 0.0)
+    return a * a * a, b * b * b
+
+
+def dense_sums(left, dens_ref, root_ref, spans):
+    count = left.shape[0]
+    near = jnp.zeros((count, 128), jnp.float32)
+    far = jnp.zeros((count, 128), jnp.float32)
+    for line, lanes, cells in spans:
+        s = product(left, dens_ref[line, :, lanes])
+        a, b = spline(s, tiled(root_ref[line, :, lanes], count // 8))
+        for k in range(cells):
+            far = far + a[:, k * 128 : (k + 1) * 128]
+            near = near + b[:, k * 128 : (k + 1) * 128]
+    return 2.0 * far - near
+
+
+def row_sums(left, dens_ref, root_ref, spans):
+    sums = [
+        dense_sums(left[k : k + ROWS], dens_ref, root_ref, spans) for k in range(0, 128, ROWS)
+    ]
+    return jnp.sum(jnp.concatenate(sums, axis=0).T, axis=0, keepdims=True)
+
+
+def density_tables(dens_ref, root_ref, line, z, fields, spot, square):
+    root = cube_root(fields[3:4])
+    part = slice(z * 128, (z + 1) * 128)
+    dens_ref[line, :, part] = source_rows(spot, square, root * root).astype(jnp.bfloat16)
+    root_ref[line, :, part] = jnp.broadcast_to(root, (8, 128))
+
+
+def lane_runs(cells, first):
+    runs = []
+    for z in cells:
+        if runs and runs[-1][1] == z:
+            runs[-1][1] = z + 1
+        else:
+            runs.append([z, z + 1])
+    return [(slice((a - first) * 128, (b - first) * 128), b - a) for a, b in runs]
+
+
+def early_kernel(src_ref, len_ref, sum_ref, dens_ref, root_ref, *, sizes, crossing):
+    nx, ny, nz = sizes
+    cx, cy, cz = nx - 2, ny - 2, nz - 2
+    columns = (0, ny - 1) if crossing else tuple(range(1, ny - 1))
+    shift = 0 if crossing else 1
+    for x, y, z in cells_of((nx, len(columns), cz)):
+        fields = src_ref[x, columns[y] - shift, z]
+        spot, square = place(fields, origin_of((x, columns[y], z + 1), sizes))
+        density_tables(dens_ref, root_ref, x * len(columns) + y, z, fields, spot, square)
+
+    def one_plane(x, carry):
+        for y in range(cy):
+            for z in range(cz):
+                fields = src_ref[x + 1, y + 1 - shift, z]
+                where = [x.astype(jnp.float32) + (1.0 - 0.5 * nx)]
+                where += [y + 1.0 - 0.5 * ny, z + 1.0 - 0.5 * nz]
+                spot, square = place(fields, where)
+                inverse = 1.0 / len_ref[x, y, z : z + 1, :]
+                left = target_rows(spot, square, inverse * inverse).T.astype(jnp.bfloat16)
+                spans = []
+                for dx in range(3):
+                    for at, source in enumerate(columns):
+                        if abs(source - y - 1) <= 1:
+                            for lanes, cells in lane_runs(near_of(z + 1, cz), 0):
+                                spans.append(((x + dx) * len(columns) + at, lanes, cells))
+                total = jnp.zeros((1, 128), jnp.float32)
+                if spans:
+                    total = row_sums(left, dens_ref, root_ref, spans)
+                sum_ref[(x * cy + y) * cz + z] = jnp.broadcast_to(total, (8, 128))
+        return carry
+
+    lax.fori_loop(0, cx, one_plane, 0)
+
+
 def half_up(count):
     return jnp.floor((count + 1.0) * 0.5)
 
 
-def sort_kernel(src_ref, side_ref, *, local):
+def sort_kernel(src_ref, act_ref, side_ref, *, local):
     row = row_index()
     across = lax.broadcasted_iota(jnp.int32, (128, 128), 0)
     along = lax.broadcasted_iota(jnp.int32, (128, 128), 1)
@@ -140,7 +224,10 @@
         slot = jnp.where(heavy > 0.0, -1.0, 16.0 * group + place_in)
         side = jnp.where(row == 0, bits[0], jnp.where(row == 1, bits[1], bits[2]))
         side = jnp.where(row == 3, heavy, side)
-        side_ref[index] = jnp.where(row == 4, slot, side)
+        side = jnp.where(row == 4, slot, side)
+        x, y, z = cell
+        active = act_ref[x, y, z : z + 1, :].astype(jnp.float32)
+        side_ref[index] = jnp.where(row == 5, active, side)
 
 
 def halves_of(source, count):
@@ -167,11 +254,14 @@
     src_ref,
     len_ref,
     side_ref,
-    act_ref,
+    early_ref,
+    second_ref,
     rho_ref,
     push_ref,
     heat_ref,
-    out_ref,
+    inner_ref,
+    low_ref,
+    high_ref,
     dens_ref,
     root_ref,
     flat_ref,
@@ -200,18 +290,15 @@
     along = lax.broadcasted_iota(jnp.int32, (128, 128), 1)
     before = jnp.where(across < along, 1.0, 0.0).astype(jnp.bfloat16)
     slot_of = across.astype(jnp.float32)
-    first16 = lax.broadcasted_iota(jnp.int32, (16, 128), 0).astype(jnp.float32)
 
     for x, y, z in cells_of(sizes):
         fields = src_ref[x, y, z]
         spot, square = place(fields, origin_of((x, y, z), sizes))
         mass = fields[3:4]
-        root = cube_root(mass)
         line = x * ny + y
         part = slice(z * 128, (z + 1) * 128)
-        dens_ref[line, :, part] = source_rows(spot, square, root * root).astype(jnp.bfloat16)
+        density_tables(dens_ref, root_ref, line, z, fields, spot, square)
         flat_ref[line, :, part] = source_rows(spot, square, 1.0).astype(jnp.bfloat16)
-        root_ref[line, :, part] = jnp.broadcast_to(root, (8, 128))
         moving = jnp.sum(fields[4:7] * spot[0:3], axis=0, keepdims=True)
         basis = jnp.where(row < 3, spot, jnp.where(row == 3, 1.0, fields))
         basis = jnp.where(row == 7, moving, basis) * mass
@@ -219,46 +306,32 @@
         col_ref[line, z * 256 : z * 256 + 128, :] = cols
         col_ref[line, z * 256 + 128 : z * 256 + 256, :] = cols
 
-    def spline(s, root):
-        s = jnp.maximum(s, TINY)
-        scaled = s * lax.rsqrt(s)
-        t = root - scaled
-        a = jnp.maximum(t, 0.0)
-        b = jnp.maximum(t - scaled, 0.0)
-        return a * a * a, b * b * b
-
-    def dense_sums(left, x, y, z):
-        count = left.shape[0]
-        near = jnp.zeros((count, 128), jnp.float32)
-        far = jnp.zeros((count, 128), jnp.float32)
-        lanes = pl.ds(pl.multiple_of(z * 128, 128), 384)
-        for dx in range(3):
-            for dy in range(3):
-                line = (x + dx) * ny + y + dy
-                s = product(left, dens_ref[line, :, lanes])
-                a, b = spline(s, tiled(root_ref[line, :, lanes], count // 8))
-                for k in range(3):
-                    far = far + a[:, k * 128 : (k + 1) * 128]
-                    near = near + b[:, k * 128 : (k + 1) * 128]
-        return 2.0 * far - near
-
-    def first_pass(index, carry):
-        x = index // (cy * cz)
-        y = index // cz % cy
-        z = index % cz
-        fields = src_ref[x + 1, y + 1, z + 1]
-        where = [v.astype(jnp.float32) + (1.0 - 0.5 * n) for v, n in zip((x, y, z), sizes)]
-        spot, square = place(fields, where)
-        inverse = 1.0 / len_ref[x, y, pl.ds(z, 1), :]
-        left = target_rows(spot, square, inverse * inverse).T.astype(jnp.bfloat16)
-        sums = [dense_sums(left[k : k + ROWS], x, y, z) for k in range(0, 128, ROWS)]
-        total = jnp.sum(jnp.concatenate(sums, axis=0).T, axis=0, keepdims=True)
-        density = kernel_norm * total * (inverse * inverse * inverse)
-        length = eta_factor * cube_root(fields[3:4] / density)
-        size_ref[index] = jnp.broadcast_to(length, (8, 128))
+    def first_pass(x, carry):
+        for y in range(cy):
+            for z in range(cz):
+                index = (x * cy + y) * cz + z
+                fields = src_ref[x + 1, y + 1, z + 1]
+                where = [x.astype(jnp.float32) + (1.0 - 0.5 * nx)]
+                where += [y + 1.0 - 0.5 * ny, z + 1.0 - 0.5 * nz]
+                spot, square = place(fields, where)
+                inverse = 1.0 / len_ref[x, y, z : z + 1, :]
+                left = target_rows(spot, square, inverse * inverse).T.astype(jnp.bfloat16)
+                spans = []
+                for dx in range(3):
+                    for source in range(y, y + 3):
+                        known = [c + 1 for c in near_of(z + 1, cz)]
+                        rest = [c for c in range(z, z + 3) if c not in known]
+                        for lanes, cells in lane_runs(rest, 0):
+                            spans.append(((x + dx) * ny + source, lanes, cells))
+                total = early_ref[index][0:1] + second_ref[index][0:1]
+                if spans:
+                    total += row_sums(left, dens_ref, root_ref, spans)
+                density = kernel_norm * total * (inverse * inverse * inverse)
+                length = eta_factor * cube_root(fields[3:4] / density)
+                size_ref[index] = jnp.broadcast_to(length, (8, 128))
         return carry
 
-    lax.fori_loop(0, cx * cy * cz, first_pass, 0)
+    lax.fori_loop(0, cx, first_pass, 0)
 
     def cell_runs(cell):
         x, y, z = cell
@@ -268,7 +341,7 @@
             for by in range(2)
         ]
 
-    def scatter_rows(ref, index, cell, value):
+    def scatter_rows(ref, cell, value):
         for k, start in enumerate(cell_runs(cell)):
             ref[start : start + 32, :] = value[k * 32 : (k + 1) * 32]
 
@@ -287,31 +360,35 @@
         slot = jnp.where(wide > 0.0, -1.0, side[4:5])
         oct_ref[index] = jnp.where(slot_of == slot, 1.0, 0.0).astype(jnp.bfloat16)
         rest_ref[index] = jnp.broadcast_to(order, (8, 128))
-        return picked(index, 0)
-
-    def picked(index, chunk):
-        order = rest_ref[index][0:1]
-        shift = jnp.float32(16.0) * chunk
-        return jnp.where(first16 + shift == order, 1.0, 0.0)
+
+    def picked(index, first, count):
+        order = rest_ref[index][0:1] - first
+        slots = lax.broadcasted_iota(jnp.int32, (count, 128), 0).astype(jnp.float32)
+        return jnp.where(slots == order, 1.0, 0.0)
 
     def set_rows(index, cell, fields, spot, square, length, weight):
         inverse = 1.0 / length
-        rest = choose(index, fields, length).astype(jnp.bfloat16)
+        choose(index, fields, length)
+        count = 16 if weight is None else WIDE
+        rest = picked(index, 0.0, count).astype(jnp.bfloat16)
         left = target_rows(spot, square, inverse * inverse).astype(jnp.bfloat16)
         chosen = oct_ref[index]
-        scatter_rows(left_ref, index, cell, product_nt(chosen, left).astype(jnp.bfloat16))
-        part = slice(inner + index * 16, inner + index * 16 + 16)
+        scatter_rows(left_ref, cell, product_nt(chosen, left).astype(jnp.bfloat16))
+        part = slice(inner + index * WIDE, inner + index * WIDE + count)
         left_ref[part, :] = product_nt(rest, left).astype(jnp.bfloat16)
         if weight is not None:
             feat = jnp.concatenate(split3(weight), axis=0).astype(jnp.bfloat16)
-            scatter_rows(feat_ref, index, cell, product_nt(chosen, feat).astype(jnp.bfloat16))
+            scatter_rows(feat_ref, cell, product_nt(chosen, feat).astype(jnp.bfloat16))
             feat_ref[part, :] = product_nt(rest, feat).astype(jnp.bfloat16)
 
-    def source_runs(x, y, z):
+    def source_runs(x, y, z, count):
         ranges = [halves_of(s, n) for s, n in zip((x, y, z), local)]
         runs = runs_of(ranges, halves)
         ranges = [near_of(s, n) for s, n in zip((x, y, z), local)]
-        return runs + [(inner + start, size) for start, size in runs_of(ranges, local)]
+        for start, size in runs_of(ranges, local):
+            for first in range(start // 16, (start + size) // 16):
+                runs.append((inner + first * WIDE, count))
+        return runs
 
     def rows_of(ref, runs):
         return jnp.concatenate([ref[start : start + size, :] for start, size in runs], axis=0)
@@ -325,10 +402,10 @@
     def unsorted_column(index, octant, rest):
         total = jnp.sum(octant, axis=1, keepdims=True) * oct_ref[index].astype(jnp.float32)
         total = jnp.sum(total, axis=0, keepdims=True)
-        rest = jnp.sum(rest, axis=1, keepdims=True) * picked(index, 0)
+        rest = jnp.sum(rest, axis=1, keepdims=True) * picked(index, 0.0, 16)
         return total + jnp.sum(rest, axis=0, keepdims=True)
 
-    def extras(visit):
+    def extras(visit, first):
         def one_cell(index, carry):
             def one_chunk(chunk, carry):
                 x = index // (cy * cz)
@@ -338,13 +415,13 @@
                 where = [v.astype(jnp.float32) + (1.0 - 0.5 * n) for v, n in zip((x, y, z), sizes)]
                 spot, square = place(fields, where)
                 inverse = 1.0 / size_ref[index][0:1]
-                rest = picked(index, chunk.astype(jnp.float32))
+                rest = picked(index, chunk.astype(jnp.float32) * 16.0, 16)
                 left = target_rows(spot, square, inverse * inverse).astype(jnp.bfloat16)
                 left = product_nt(rest.astype(jnp.bfloat16), left).astype(jnp.bfloat16)
                 visit(index, (x, y, z), fields, spot, rest, left)
                 return carry
 
-            return lax.fori_loop(1, (count_ref[index] + 15) // 16, one_chunk, carry)
+            return lax.fori_loop(first, (count_ref[index] + 15) // 16, one_chunk, carry)
 
         lax.fori_loop(0, cx * cy * cz, one_cell, 0)
 
@@ -352,7 +429,11 @@
         return jnp.where(row < 3, spot, jnp.where(row == 3, 1.0, 0.0)) * (fields[3:4] * strength)
 
     def extra_density(index, cell, fields, spot, rest, left):
-        extra = jnp.sum(dense_sums(left, *cell), axis=1, keepdims=True) * rest
+        x, y, z = cell
+        lanes = pl.ds(pl.multiple_of(z * 128, 128), 384)
+        spans = [((x + dx) * ny + y + dy, lanes, 3) for dx in range(3) for dy in range(3)]
+        extra = dense_sums(left, dens_ref, root_ref, spans)
+        extra = jnp.sum(extra, axis=1, keepdims=True) * rest
         sum_ref[index, 0:8, :] += jnp.sum(extra, axis=0, keepdims=True)
 
     def unsort(value, rest):
@@ -392,7 +473,7 @@
     far_ref[...] = jnp.zeros_like(far_ref)
     close_ref[...] = jnp.zeros_like(close_ref)
     for x, y, z in cells_of(sizes):
-        runs = source_runs(x, y, z)
+        runs = source_runs(x, y, z, 16)
         line = x * ny + y
         part = slice(z * 128, (z + 1) * 128)
         left = rows_of(left_ref, runs)
@@ -402,14 +483,14 @@
         add_rows(close_ref, runs, b)
 
     for index, cell in enumerate(cells):
-        part = slice(inner + index * 16, inner + index * 16 + 16)
+        part = slice(inner + index * WIDE, inner + index * WIDE + 16)
         octant = gather_rows(
             lambda start: 2.0 * far_ref[start : start + 32, :] - close_ref[start : start + 32, :],
             cell,
         )
         total = unsorted_column(index, octant, 2.0 * far_ref[part, :] - close_ref[part, :])
         sum_ref[index, 0:8, :] = jnp.broadcast_to(total, (8, 128))
-    extras(extra_density)
+    extras(extra_density, 1)
     for index, cell in enumerate(cells):
         x, y, z = cell
         fields, origin = placed[index]
@@ -418,14 +499,14 @@
         density = kernel_norm * sum_ref[index, 0:1, :] * (inverse * inverse * inverse)
         rho_ref[x, y, z : z + 1, :] = density
         length = eta_factor * cube_root(fields[3:4] / density)
-        inv2, strength = smooth(fields, density)
+        _, strength = smooth(fields, density)
         size_ref[index] = jnp.where(row == 0, length, strength)
         set_rows(index, cell, fields, spot, square, length, weight_of(fields, spot, strength))
 
     own_ref[...] = jnp.zeros_like(own_ref)
 
     def slopes(x, y, z):
-        runs = source_runs(x, y, z)
+        runs = source_runs(x, y, z, WIDE)
         line = x * ny + y
         part = slice(z * 128, (z + 1) * 128)
         high, low = profile(product(rows_of(left_ref, runs), flat_ref[line, :, part]))
@@ -448,17 +529,17 @@
 
     for index, cell in enumerate(cells):
         octant = gather_rows(lambda start: own_ref[start : start + 32, :], cell)
-        part = slice(inner + index * 16, inner + index * 16 + 16)
-        own = unsort(octant, oct_ref[index]) + unsort(own_ref[part, :], picked(index, 0))
+        part = slice(inner + index * WIDE, inner + index * WIDE + WIDE)
+        own = unsort(octant, oct_ref[index]) + unsort(own_ref[part, :], picked(index, 0.0, WIDE))
         sum_ref[index] = own
-    extras(extra_force)
+    extras(extra_force, WIDE // 16)
     for index, cell in enumerate(cells):
         x, y, z = cell
         fields, origin = placed[index]
         spot, square = place(fields, origin)
         own = sum_ref[index]
         own = (own[0:8] + own[8:16] + own[16:24]) * size_ref[index][1:2]
-        active = act_ref[x, y, z : z + 1, :].astype(jnp.float32)
+        active = side_ref[index, 5:6, :]
         spot = spot[0:3]
         push = spot * own[3:4] - own[0:3]
         heat = fields[4:7] * push - spot * own[4:7]
@@ -470,7 +551,13 @@
         spot, square = place(src_ref[x, y, z], origin_of((x, y, z), sizes))
         their = their_ref[x * ny + y, :, z * 128 : (z + 1) * 128]
         their = their[0:8] + their[8:16] + their[16:24]
-        out_ref[x, y, z] = (spot * their[3:4] - their)[0:4]
+        their = (spot * their[3:4] - their)[0:4]
+        if z == 0:
+            low_ref[x, y, 0] = their
+        elif z == nz - 1:
+            high_ref[x, y, 0] = their
+        else:
+            inner_ref[x, y, z - 1] = their
 
 
 def profile(s):
@@ -496,19 +583,20 @@
     return lax.slice_in_dim(block, start, stop, axis=dim)
 
 
-def fold(block):
+def fold(block, low, high):
     for dim in (2, 1, 0):
         axis = AXES[dim]
-        last = block.shape[dim] - 1
-        low, high = take(block, dim, 0, 1), take(block, dim, last, last + 1)
+        if dim < 2:
+            last = block.shape[dim] - 1
+            low, high = take(block, dim, 0, 1), take(block, dim, last, last + 1)
+            block = take(block, dim, 1, last)
         if lax.axis_size(axis) == 2:
             both = lax.ppermute(jnp.concatenate([high, low], axis=dim), axis, ring(axis, 1))
             to_first, to_last = take(both, dim, 0, 1), take(both, dim, 1, 2)
         else:
             to_last = lax.ppermute(low, axis, ring(axis, -1))
             to_first = lax.ppermute(high, axis, ring(axis, 1))
-        block = take(block, dim, 1, last)
-        count = last - 1
+        count = block.shape[dim]
         if count == 1:
             block = block + to_first + to_last
         else:
@@ -539,17 +627,36 @@
         out_shape=jax.ShapeDtypeStruct((ncell, 8, 128), f32),
         compiler_params=pltpu.CompilerParams(vmem_limit_bytes=VMEM_LIMIT),
         name="sort",
-    )(static)
-    padded = halo(static)
+    )(static, active)
+    wide = halo(static, (0,))
+
+    def begin(block, crossing):
+        lines = nx * (2 if crossing else local[1])
+        return pl.pallas_call(
+            functools.partial(early_kernel, sizes=sizes, crossing=crossing),
+            out_shape=jax.ShapeDtypeStruct((ncell, 8, 128), f32),
+            scratch_shapes=[
+                pltpu.VMEM((lines, 48, local[2] * 128), bf16),
+                pltpu.VMEM((lines, 8, local[2] * 128), f32),
+            ],
+            compiler_params=pltpu.CompilerParams(vmem_limit_bytes=VMEM_LIMIT),
+        )(block, smoothing)
+
+    early = begin(wide, False)
+    tall = halo(wide, (1,))
+    second = begin(tall, True)
+    padded = halo(tall, (2,))
     lines = nx * ny
-    rows = ncell * 144
-    density, push, heat, spread = pl.pallas_call(
+    rows = ncell * (128 + WIDE)
+    density, push, heat, spread, low, high = pl.pallas_call(
         functools.partial(main_kernel, sizes=sizes),
         out_shape=(
             jax.ShapeDtypeStruct(masses.shape, f32),
             jax.ShapeDtypeStruct(local + (4, 128), f32),
             jax.ShapeDtypeStruct(masses.shape, f32),
-            jax.ShapeDtypeStruct(sizes + (4, 128), f32),
+            jax.ShapeDtypeStruct((nx, ny, local[2], 4, 128), f32),
+            jax.ShapeDtypeStruct((nx, ny, 1, 4, 128), f32),
+            jax.ShapeDtypeStruct((nx, ny, 1, 4, 128), f32),
         ),
         scratch_shapes=[
             pltpu.VMEM((lines, 48, nz * 128), bf16),
@@ -570,8 +677,8 @@
         ],
         compiler_params=pltpu.CompilerParams(vmem_limit_bytes=VMEM_LIMIT),
         name="main",
-    )(padded, smoothing, side, active)
-    total = -(push[..., 0:3, :] + fold(spread)[..., 0:3, :]) * push[..., 3:4, :]
+    )(padded, smoothing, side, early, second)
+    total = -(push[..., 0:3, :] + fold(spread, low, high)[..., 0:3, :]) * push[..., 3:4, :]
     return (density, jnp.moveaxis(total, 3, 0), heat)
 
 

time: 88 us -> 78.2 us (0.89); the launches traced: 89 us -> 77.8 us
  starting transfers between devices: 44.8 us -> 29 us
  Pallas kernels: 25.9 us -> 31.4 us
    ppermute x1, starting transfers between devices: 18.9 us -> 2.03 us  [fold(): lax.ppermute(jnp.concatenate([high, low], axis=dim), axis, ring(axis, 1))]
    ppermute x2, starting transfers between devices: 9.37 us -> 17 us  [fold(): to_last = lax.ppermute(low, axis, ring(axis, -1))]
    ppermute x2, starting transfers between devices: 7.46 us -> 0.86 us  [fold(): to_first = lax.ppermute(high, axis, ring(axis, 1))]
    pallas_call x0 -> x2, Pallas kernels: none -> 6.07 us  [begin(): pl.pallas_call(functools.partial(early_kernel, sizes=sizes, crossing=cros...]
    ppermute x2, waiting for transfers between devices: 6.38 us -> 2.9 us  [fold(): to_last = lax.ppermute(low, axis, ring(axis, -1))]
    ppermute x2, waiting for transfers between devices: 2.51 us -> 5.69 us  [fold(): to_first = lax.ppermute(high, axis, ring(axis, 1))]
  transfers between devices with their start and end apart: 10 -> 10, of which waited for: 7 -> 8; matrix products, arithmetic and copies ran while one was open for 0% -> 0% of each run, Pallas kernels for 3% -> 12%
where the time goes in v2:
time: 78.2 us; the launch traced here: 77.8 us
  Pallas kernels  31.4 us (40%)
  starting transfers between devices  29 us (37%)
  waiting for transfers between devices  14.4 us (18%)
  local copies, waits for them, and re-layouts  2.13 us (3%)
    pallas_call x1, Pallas kernels, body(): pl.pallas_call(functools.partial(main_kernel, sizes=sizes), out_shape=(ja...  22.4 us
    ppermute x2, starting transfers between devices, fold(): to_last = lax.ppermute(low, axis, ring(axis, -1))  17 us
    ppermute x5, starting transfers between devices, move(): return lax.ppermute(block, axis, ring(axis, step))  9.06 us
    pallas_call x2, Pallas kernels, begin(): pl.pallas_call(functools.partial(early_kernel, sizes=sizes, crossing=cros...  6.07 us
    ppermute x2, waiting for transfers between devices, fold(): to_first = lax.ppermute(high, axis, ring(axis, 1))  5.69 us
    ppermute x5, waiting for transfers between devices, move(): return lax.ppermute(block, axis, ring(axis, step))  4.07 us
    pallas_call x1, Pallas kernels, body(): pl.pallas_call(functools.partial(sort_kernel, local=local), out_shape=jax...  2.95 us
    ppermute x2, waiting for transfers between devices, fold(): to_last = lax.ppermute(low, axis, ring(axis, -1))  2.9 us
  transfers between devices with their start and end apart: 10, of which 8 were waited for; matrix products, arithmetic and copies ran while one was open for 0% of the time, Pallas kernels for 12%

profile of v2, /device:TPU:0, one launch (start us, length us, event | category | flops | bytes accessed | tf_op | source)
XLA Modules:
  0.0 77.8 jit_solution(15649213475823526295)
XLA Ops:
  0.6 0.7 fusion.17
  1.4 0.0 copy-start.3
  1.4 0.7 copy-done.4
  2.1 0.0 copy-done.3
  2.1 0.1 stack.11.src_ref
  2.1 3.0 %collective-permute-start = (f32[2,2,2,8,128]{4,3,2,1,0:T(8,128)S(1)}, f32[2,2,2,8,128]{4,3,2,1,0:T(8,128)S(1)}, u32[]{:S(2)}, u32[]{:S(2)}) collective-permute-start(f32[2,2,2,8,128]{4,3,2,1,0:T(8,128)S(1)} %stack.11.src_ref), channel_id=1, source_target_pairs={{0,16},{16,0},{1,17},{17,1},{2,18},{18,2},{3,19},{19,3},{4,20},{20... | collective-permute-start | bytes 98312 | tf_op jit(solution)/shard_map/ppermute | solution.py:28
  5.2 1.9 %collective-permute-done = f32[2,2,2,8,128]{4,3,2,1,0:T(8,128)S(1)} collective-permute-done((f32[2,2,2,8,128]{4,3,2,1,0:T(8,128)S(1)}, f32[2,2,2,8,128]{4,3,2,1,0:T(8,128)S(1)}, u32[]{:S(2)}, u32[]{:S(2)}) %collective-permute-start) | collective-permute-done | bytes 32800 | tf_op jit(solution)/shard_map/ppermute | solution.py:28
  7.1 2.2 %collective-permute-start.1 = (f32[4,1,2,8,128]{4,3,2,1,0:T(8,128)S(1)}, f32[4,1,2,8,128]{4,3,2,1,0:T(8,128)S(1)}, u32[]{:S(2)}, u32[]{:S(2)}) collective-permute-start(f32[4,1,2,8,128]{4,3,2,1,0:T(8,128)S(1)} %get-tuple-element.26), channel_id=1, source_target_pairs={{0,4},{4,8},{8,12},{12,0},{1,5},{5,9},{9,13},{13,1},{2,6},{6,10},{... | collective-permute-start | bytes 98312 | tf_op jit(solution)/shard_map/ppermute | solution.py:28
  9.2 2.1 %collective-permute-start.2 = (f32[4,1,2,8,128]{4,3,2,1,0:T(8,128)S(1)}, f32[4,1,2,8,128]{4,3,2,1,0:T(8,128)S(1)}, u32[]{:S(2)}, u32[]{:S(2)}) collective-permute-start(f32[4,1,2,8,128]{4,3,2,1,0:T(8,128)S(1)} %get-tuple-element.27), channel_id=1, source_target_pairs={{0,12},{4,0},{8,4},{12,8},{1,13},{5,1},{9,5},{13,9},{2,14},{6,2},{... | collective-permute-start | bytes 98312 | tf_op jit(solution)/shard_map/ppermute | solution.py:28
  11.3 1.9 %collective-permute-done.1 = f32[4,1,2,8,128]{4,3,2,1,0:T(8,128)S(1)} collective-permute-done((f32[4,1,2,8,128]{4,3,2,1,0:T(8,128)S(1)}, f32[4,1,2,8,128]{4,3,2,1,0:T(8,128)S(1)}, u32[]{:S(2)}, u32[]{:S(2)}) %collective-permute-start.1) | collective-permute-done | bytes 32800 | tf_op jit(solution)/shard_map/ppermute | solution.py:28
  13.3 0.2 collective-permute-done.2
  13.5 0.0 copy-start.1
  13.6 0.1 collective-permute-start.3
  13.6 0.0 copy-start
  13.6 1.7 %collective-permute-start.4 = (f32[4,4,1,8,128]{4,3,2,1,0:T(8,128)S(1)}, f32[4,4,1,8,128]{4,3,2,1,0:T(8,128)S(1)}, u32[]{:S(2)}, u32[]{:S(2)}) collective-permute-start(f32[4,4,1,8,128]{4,3,2,1,0:T(8,128)S(1)} %get-tuple-element.19), channel_id=1, source_target_pairs={{0,3},{1,0},{2,1},{3,2},{4,7},{5,4},{6,5},{7,6},{8,11},{9,8},{10,9... | collective-permute-start | bytes 196616 | tf_op jit(solution)/shard_map/ppermute | solution.py:28
  15.4 2.9 %sort.1.side_ref = f32[8,8,128]{2,1,0:T(8,128)S(1)} custom-call(f32[2,2,2,8,128]{4,3,2,1,0:T(8,128)S(1)} %stack.11.src_ref, s32[2,2,2,128]{3,2,1,0:T(2,128)S(1)} %copy-done.1), custom_call_target="tpu_custom_call" | custom-call | tf_op jit(solution)/shard_map/sort/pallas_call | solution.py:625
  18.3 3.8 %shard_map.85.early_ref = f32[8,8,128]{2,1,0:T(8,128)S(1)} custom-call(f32[4,2,2,8,128]{4,3,2,1,0:T(8,128)S(1)} %pad_maximum_fusion.2.src_ref, f32[2,2,2,128]{3,2,1,0:T(2,128)S(1)} %copy-done), custom_call_target="tpu_custom_call" | custom-call | tf_op jit(solution)/shard_map/pallas_call | solution.py:635
  22.2 2.2 %shard_map.86.second_ref = f32[8,8,128]{2,1,0:T(8,128)S(1)} custom-call(f32[4,4,2,8,128]{4,3,2,1,0:T(8,128)S(1)} %pad_maximum_fusion.1.src_ref, f32[2,2,2,128]{3,2,1,0:T(2,128)S(1)} %copy-done), custom_call_target="tpu_custom_call" | custom-call | tf_op jit(solution)/shard_map/pallas_call | solution.py:635
  24.4 0.0 collective-permute-done.3
  24.4 0.0 collective-permute-done.4
  24.5 22.4 %main.1 = (f32[2,2,2,128]{3,2,1,0:T(2,128)}, f32[2,2,2,4,128]{4,3,2,1,0:T(4,128)S(1)}, f32[2,2,2,128]{3,2,1,0:T(2,128)}, f32[4,4,2,4,128]{4,3,2,1,0:T(4,128)S(1)...) custom-call(f32[4,4,4,8,128]{4,3,2,1,0:T(8,128)S(1)} %pad_maximum_fusion.src_ref, ...), custom_call_target="tpu_custom_call" | custom-call | tf_op jit(solution)/shard_map/main/pallas_call | solution.py:651
  46.8 0.9 %collective-permute-start.5 = (f32[4,4,1,4,128]{4,3,2,1,0:T(4,128)S(1)}, f32[4,4,1,4,128]{4,3,2,1,0:T(4,128)S(1)}, u32[]{:S(2)}, u32[]{:S(2)}) collective-permute-start(f32[4,4,1,4,128]{4,3,2,1,0:T(4,128)S(1)} %get-tuple-element.12), channel_id=1, source_target_pairs={{0,1},{1,2},{2,3},{3,0},{4,5},{5,6},{6,7},{7,4},{8,9},{9,10},{10,1... | collective-permute-start | bytes 98312 | tf_op jit(solution)/shard_map/ppermute | solution.py:598
  47.7 0.9 %collective-permute-start.6 = (f32[4,4,1,4,128]{4,3,2,1,0:T(4,128)S(1)}, f32[4,4,1,4,128]{4,3,2,1,0:T(4,128)S(1)}, u32[]{:S(2)}, u32[]{:S(2)}) collective-permute-start(f32[4,4,1,4,128]{4,3,2,1,0:T(4,128)S(1)} %get-tuple-element.13), channel_id=1, source_target_pairs={{0,3},{1,0},{2,1},{3,2},{4,7},{5,4},{6,5},{7,6},{8,11},{9,8},{10,9... | collective-permute-start | bytes 98312 | tf_op jit(solution)/shard_map/ppermute | solution.py:597
  48.6 1.6 %collective-permute-done.5 = f32[4,4,1,4,128]{4,3,2,1,0:T(4,128)S(1)} collective-permute-done((f32[4,4,1,4,128]{4,3,2,1,0:T(4,128)S(1)}, f32[4,4,1,4,128]{4,3,2,1,0:T(4,128)S(1)}, u32[]{:S(2)}, u32[]{:S(2)}) %collective-permute-start.5) | collective-permute-done | bytes 32800 | tf_op jit(solution)/shard_map/ppermute | solution.py:598
  50.1 1.5 %collective-permute-done.6 = f32[4,4,1,4,128]{4,3,2,1,0:T(4,128)S(1)} collective-permute-done((f32[4,4,1,4,128]{4,3,2,1,0:T(4,128)S(1)}, f32[4,4,1,4,128]{4,3,2,1,0:T(4,128)S(1)}, u32[]{:S(2)}, u32[]{:S(2)}) %collective-permute-start.6) | collective-permute-done | bytes 32800 | tf_op jit(solution)/shard_map/ppermute | solution.py:597
  51.6 16.2 %collective-permute-start.8 = (f32[4,1,2,4,128]{4,3,2,1,0:T(4,128)S(1)}, f32[4,1,2,4,128]{4,3,2,1,0:T(4,128)S(1)}, u32[]{:S(2)}, u32[]{:S(2)}) collective-permute-start(f32[4,1,2,4,128]{4,3,2,1,0:T(4,128)S(1)} %get-tuple-element.22), channel_id=1, source_target_pairs={{0,12},{4,0},{8,4},{12,8},{1,13},{5,1},{9,5},{13,9},{2,14},{6,2},{... | collective-permute-start | bytes 49160 | tf_op jit(solution)/shard_map/ppermute | solution.py:597
  67.8 0.0 collective-permute-start.7
  67.8 1.4 %collective-permute-done.8 = f32[4,1,2,4,128]{4,3,2,1,0:T(4,128)S(1)} collective-permute-done((f32[4,1,2,4,128]{4,3,2,1,0:T(4,128)S(1)}, f32[4,1,2,4,128]{4,3,2,1,0:T(4,128)S(1)}, u32[]{:S(2)}, u32[]{:S(2)}) %collective-permute-start.8) | collective-permute-done | bytes 16416 | tf_op jit(solution)/shard_map/ppermute | solution.py:597
  69.3 4.1 %collective-permute-done.7 = f32[4,1,2,4,128]{4,3,2,1,0:T(4,128)S(1)} collective-permute-done((f32[4,1,2,4,128]{4,3,2,1,0:T(4,128)S(1)}, f32[4,1,2,4,128]{4,3,2,1,0:T(4,128)S(1)}, u32[]{:S(2)}, u32[]{:S(2)}) %collective-permute-start.7) | collective-permute-done | bytes 16416 | tf_op jit(solution)/shard_map/ppermute | solution.py:598
  73.4 2.0 %collective-permute-start.9 = (f32[2,2,2,4,128]{4,3,2,1,0:T(4,128)S(1)}, f32[2,2,2,4,128]{4,3,2,1,0:T(4,128)S(1)}, u32[]{:S(2)}, u32[]{:S(2)}) collective-permute-start(f32[2,2,2,4,128]{4,3,2,1,0:T(4,128)S(1)} %pad_maximum_fusion.5), channel_id=1, source_target_pairs={{0,16},{16,0},{1,17},{17,1},{2,18},{18,2},{3,19},{19,3},{4,20},{20... | collective-permute-start | bytes 49160 | tf_op jit(solution)/shard_map/ppermute | solution.py:594
  75.4 1.8 %collective-permute-done.9 = f32[2,2,2,4,128]{4,3,2,1,0:T(4,128)S(1)} collective-permute-done((f32[2,2,2,4,128]{4,3,2,1,0:T(4,128)S(1)}, f32[2,2,2,4,128]{4,3,2,1,0:T(4,128)S(1)}, u32[]{:S(2)}, u32[]{:S(2)}) %collective-permute-start.9) | collective-permute-done | bytes 16416 | tf_op jit(solution)/shard_map/ppermute | solution.py:594
  77.2 0.6 copy.9
  (20 shorter events, 0.2 us)
Async XLA Ops:
  0.6 0.7 copy-start.2
  1.4 0.7 copy-start.4
  1.4 0.7 copy-start.3
  2.1 4.9 %collective-permute-start = (f32[2,2,2,8,128]{4,3,2,1,0:T(8,128)S(1)}, f32[2,2,2,8,128]{4,3,2,1,0:T(8,128)S(1)}, u32[]{:S(2)}, u32[]{:S(2)}) collective-permute-start(f32[2,2,2,8,128]{4,3,2,1,0:T(8,128)S(1)} %stack.11.src_ref), channel_id=1, source_target_pairs={{0,16},{16,0},{1,17},{17,1},{2,18},{18,2},{3,19},{19,3},{4,20},{20... | collective-permute-start | bytes 98312 | tf_op jit(solution)/shard_map/ppermute | solution.py:28
  7.1 6.2 %collective-permute-start.1 = (f32[4,1,2,8,128]{4,3,2,1,0:T(8,128)S(1)}, f32[4,1,2,8,128]{4,3,2,1,0:T(8,128)S(1)}, u32[]{:S(2)}, u32[]{:S(2)}) collective-permute-start(f32[4,1,2,8,128]{4,3,2,1,0:T(8,128)S(1)} %get-tuple-element.26), channel_id=1, source_target_pairs={{0,4},{4,8},{8,12},{12,0},{1,5},{5,9},{9,13},{13,1},{2,6},{6,10},{... | collective-permute-start | bytes 98312 | tf_op jit(solution)/shard_map/ppermute | solution.py:28
  9.2 4.3 %collective-permute-start.2 = (f32[4,1,2,8,128]{4,3,2,1,0:T(8,128)S(1)}, f32[4,1,2,8,128]{4,3,2,1,0:T(8,128)S(1)}, u32[]{:S(2)}, u32[]{:S(2)}) collective-permute-start(f32[4,1,2,8,128]{4,3,2,1,0:T(8,128)S(1)} %get-tuple-element.27), channel_id=1, source_target_pairs={{0,12},{4,0},{8,4},{12,8},{1,13},{5,1},{9,5},{13,9},{2,14},{6,2},{... | collective-permute-start | bytes 98312 | tf_op jit(solution)/shard_map/ppermute | solution.py:28
  13.5 1.8 %copy-start.1 = (s32[2,2,2,128]{3,2,1,0:T(2,128)S(1)}, s32[2,2,2,128]{3,2,1,0:T(2,128)}, u32[]{:S(2)}) copy-start(s32[2,2,2,128]{3,2,1,0:T(2,128)} %act_ref.1) | copy-start | bytes 12292
  13.6 10.8 %collective-permute-start.3 = (f32[4,4,1,8,128]{4,3,2,1,0:T(8,128)S(1)}, f32[4,4,1,8,128]{4,3,2,1,0:T(8,128)S(1)}, u32[]{:S(2)}, u32[]{:S(2)}) collective-permute-start(f32[4,4,1,8,128]{4,3,2,1,0:T(8,128)S(1)} %get-tuple-element.18), channel_id=1, source_target_pairs={{0,1},{1,2},{2,3},{3,0},{4,5},{5,6},{6,7},{7,4},{8,9},{9,10},{10,1... | collective-permute-start | bytes 196616 | tf_op jit(solution)/shard_map/ppermute | solution.py:28
  13.6 4.7 %copy-start = (f32[2,2,2,128]{3,2,1,0:T(2,128)S(1)}, f32[2,2,2,128]{3,2,1,0:T(2,128)}, u32[]{:S(2)}) copy-start(f32[2,2,2,128]{3,2,1,0:T(2,128)} %len_ref.5) | copy-start | bytes 12292
  13.6 10.8 %collective-permute-start.4 = (f32[4,4,1,8,128]{4,3,2,1,0:T(8,128)S(1)}, f32[4,4,1,8,128]{4,3,2,1,0:T(8,128)S(1)}, u32[]{:S(2)}, u32[]{:S(2)}) collective-permute-start(f32[4,4,1,8,128]{4,3,2,1,0:T(8,128)S(1)} %get-tuple-element.19), channel_id=1, source_target_pairs={{0,3},{1,0},{2,1},{3,2},{4,7},{5,4},{6,5},{7,6},{8,11},{9,8},{10,9... | collective-permute-start | bytes 196616 | tf_op jit(solution)/shard_map/ppermute | solution.py:28
  46.8 3.3 %collective-permute-start.5 = (f32[4,4,1,4,128]{4,3,2,1,0:T(4,128)S(1)}, f32[4,4,1,4,128]{4,3,2,1,0:T(4,128)S(1)}, u32[]{:S(2)}, u32[]{:S(2)}) collective-permute-start(f32[4,4,1,4,128]{4,3,2,1,0:T(4,128)S(1)} %get-tuple-element.12), channel_id=1, source_target_pairs={{0,1},{1,2},{2,3},{3,0},{4,5},{5,6},{6,7},{7,4},{8,9},{9,10},{10,1... | collective-permute-start | bytes 98312 | tf_op jit(solution)/shard_map/ppermute | solution.py:598
  47.7 3.9 %collective-permute-start.6 = (f32[4,4,1,4,128]{4,3,2,1,0:T(4,128)S(1)}, f32[4,4,1,4,128]{4,3,2,1,0:T(4,128)S(1)}, u32[]{:S(2)}, u32[]{:S(2)}) collective-permute-start(f32[4,4,1,4,128]{4,3,2,1,0:T(4,128)S(1)} %get-tuple-element.13), channel_id=1, source_target_pairs={{0,3},{1,0},{2,1},{3,2},{4,7},{5,4},{6,5},{7,6},{8,11},{9,8},{10,9... | collective-permute-start | bytes 98312 | tf_op jit(solution)/shard_map/ppermute | solution.py:597
  51.6 17.6 %collective-permute-start.8 = (f32[4,1,2,4,128]{4,3,2,1,0:T(4,128)S(1)}, f32[4,1,2,4,128]{4,3,2,1,0:T(4,128)S(1)}, u32[]{:S(2)}, u32[]{:S(2)}) collective-permute-start(f32[4,1,2,4,128]{4,3,2,1,0:T(4,128)S(1)} %get-tuple-element.22), channel_id=1, source_target_pairs={{0,12},{4,0},{8,4},{12,8},{1,13},{5,1},{9,5},{13,9},{2,14},{6,2},{... | collective-permute-start | bytes 49160 | tf_op jit(solution)/shard_map/ppermute | solution.py:597
  67.8 5.5 %collective-permute-start.7 = (f32[4,1,2,4,128]{4,3,2,1,0:T(4,128)S(1)}, f32[4,1,2,4,128]{4,3,2,1,0:T(4,128)S(1)}, u32[]{:S(2)}, u32[]{:S(2)}) collective-permute-start(f32[4,1,2,4,128]{4,3,2,1,0:T(4,128)S(1)} %get-tuple-element.23), channel_id=1, source_target_pairs={{0,4},{4,8},{8,12},{12,0},{1,5},{5,9},{9,13},{13,1},{2,6},{6,10},{... | collective-permute-start | bytes 49160 | tf_op jit(solution)/shard_map/ppermute | solution.py:598
  73.4 3.8 %collective-permute-start.9 = (f32[2,2,2,4,128]{4,3,2,1,0:T(4,128)S(1)}, f32[2,2,2,4,128]{4,3,2,1,0:T(4,128)S(1)}, u32[]{:S(2)}, u32[]{:S(2)}) collective-permute-start(f32[2,2,2,4,128]{4,3,2,1,0:T(4,128)S(1)} %pad_maximum_fusion.5), channel_id=1, source_target_pairs={{0,16},{16,0},{1,17},{17,1},{2,18},{18,2},{3,19},{19,3},{4,20},{20... | collective-permute-start | bytes 49160 | tf_op jit(solution)/shard_map/ppermute | solution.py:594

commit v3 on v2

--- a/solution.py
+++ b/solution.py
@@ -250,6 +250,195 @@
     ]
 
 
+def cell_runs(cell, halves):
+    x, y, z = cell
+    return [
+        (((2 * x + bx) * halves[1] + 2 * y + by) * halves[2] + 2 * z) * 16
+        for bx in range(2)
+        for by in range(2)
+    ]
+
+
+def scatter_rows(ref, cell, halves, value):
+    for k, start in enumerate(cell_runs(cell, halves)):
+        ref[start : start + 32, :] = value[k * 32 : (k + 1) * 32]
+
+
+def gather_rows(value_of, cell, halves):
+    return jnp.concatenate([value_of(start) for start in cell_runs(cell, halves)], axis=0)
+
+
+def source_runs(source, local, count):
+    inner = 128 * local[0] * local[1] * local[2]
+    ranges = [halves_of(s, n) for s, n in zip(source, local)]
+    runs = runs_of(ranges, [2 * n for n in local])
+    ranges = [near_of(s, n) for s, n in zip(source, local)]
+    for start, size in runs_of(ranges, local):
+        for first in range(start // 16, (start + size) // 16):
+            runs.append((inner + first * WIDE, count))
+    return runs
+
+
+def rows_of(ref, runs):
+    return jnp.concatenate([ref[start : start + size, :] for start, size in runs], axis=0)
+
+
+def add_rows(ref, runs, value):
+    at = 0
+    for start, size in runs:
+        ref[start : start + size, :] += value[at : at + size]
+        at += size
+
+
+def picked(rest_ref, index, first, count):
+    order = rest_ref[index][0:1] - first
+    slots = lax.broadcasted_iota(jnp.int32, (count, 128), 0).astype(jnp.float32)
+    return jnp.where(slots == order, 1.0, 0.0)
+
+
+def unsort(value, rest):
+    pieces = split3(value)
+    rest = rest.astype(jnp.bfloat16)
+    total = product_tn(pieces[0].astype(jnp.bfloat16), rest)
+    total += product_tn(pieces[1].astype(jnp.bfloat16), rest)
+    return total + product_tn(pieces[2].astype(jnp.bfloat16), rest)
+
+
+def force_columns(fields, spot):
+    row = row_index()
+    moving = jnp.sum(fields[4:7] * spot[0:3], axis=0, keepdims=True)
+    basis = jnp.where(row < 3, spot, jnp.where(row == 3, 1.0, fields))
+    basis = jnp.where(row == 7, moving, basis) * fields[3:4]
+    return jnp.concatenate(split3(basis), axis=0).T.astype(jnp.bfloat16)
+
+
+def force_sums(sources, left_ref, feat_ref, own_ref, flat_of, cols_of, put, local):
+    def sums(source, runs, high, low):
+        add_rows(own_ref, runs, product(jnp.concatenate([high, low], axis=1), cols_of(source)))
+        feat = rows_of(feat_ref, runs)
+        put(source, product_tn(feat, high) + product_tn(feat, low))
+
+    waiting = None
+    for source in sources:
+        runs = source_runs(source, local, WIDE)
+        high, low = profile(product(rows_of(left_ref, runs), flat_of(source)))
+        if waiting is not None:
+            sums(*waiting)
+        waiting = (source, runs, high, low)
+    sums(*waiting)
+
+
+def is_local(cell, local):
+    return all(0 < c <= n for c, n in zip(cell, local))
+
+
+def edge_kernel(
+    src_ref, left_ref, feat_ref, own_ref, low_ref, high_ref, flat_ref, col_ref, *, sizes, dim
+):
+    local = tuple(n - 2 for n in sizes)
+    ends = (0, sizes[dim] - 1)
+    numbers = {}
+    for cell in cells_of(sizes):
+        if cell[dim] in ends and all(0 < cell[k] <= local[k] for k in range(dim + 1, 3)):
+            if dim == 1 or is_local(cell[1:], local[1:]):
+                numbers[cell] = len(numbers)
+    for cell, index in numbers.items():
+        fields = src_ref[cell]
+        spot, square = place(fields, origin_of(cell, sizes))
+        flat_ref[index] = source_rows(spot, square, 1.0).astype(jnp.bfloat16)
+        cols = force_columns(fields, spot)
+        col_ref[index, 0:128, :] = cols
+        col_ref[index, 128:256, :] = cols
+    own_ref[...] = jnp.zeros_like(own_ref)
+
+    def put(source, value):
+        spot, _ = place(src_ref[source], origin_of(source, sizes))
+        their = value[0:8] + value[8:16] + value[16:24]
+        at = [c if k < dim else c - 1 for k, c in enumerate(source)]
+        at[dim] = 0
+        ref = low_ref if source[dim] == 0 else high_ref
+        ref[tuple(at)] = (spot * their[3:4] - their)[0:4]
+
+    force_sums(
+        list(numbers),
+        left_ref,
+        feat_ref,
+        own_ref,
+        lambda source: flat_ref[numbers[source]],
+        lambda source: col_ref[numbers[source]],
+        put,
+        local,
+    )
+
+
+def rest_kernel(
+    src_ref,
+    side_ref,
+    size_ref,
+    left_ref,
+    feat_ref,
+    oct_ref,
+    rest_ref,
+    part_ref,
+    sum_ref,
+    wide_ref,
+    tall_ref,
+    push_ref,
+    heat_ref,
+    flat_ref,
+    col_ref,
+    own_ref,
+    their_ref,
+    *,
+    sizes,
+):
+    local = tuple(n - 2 for n in sizes)
+    halves = [2 * n for n in local]
+    cells = cells_of(local)
+    inner = 128 * len(cells)
+    numbers = {tuple(c + 1 for c in cell): k for k, cell in enumerate(cells)}
+    places = []
+    for index, cell in enumerate(cells):
+        fields = src_ref[cell]
+        spot, square = place(fields, origin_of([c + 1 for c in cell], sizes))
+        flat_ref[index] = source_rows(spot, square, 1.0).astype(jnp.bfloat16)
+        cols = force_columns(fields, spot)
+        col_ref[index, 0:128, :] = cols
+        col_ref[index, 128:256, :] = cols
+        places.append((fields, spot[0:3]))
+    own_ref[...] = part_ref[...] + wide_ref[...] + tall_ref[...]
+
+    def put(source, value):
+        their_ref[numbers[source]] = value
+
+    force_sums(
+        list(numbers),
+        left_ref,
+        feat_ref,
+        own_ref,
+        lambda source: flat_ref[numbers[source]],
+        lambda source: col_ref[numbers[source]],
+        put,
+        local,
+    )
+    for index, cell in enumerate(cells):
+        fields, spot = places[index]
+        octant = gather_rows(lambda start: own_ref[start : start + 32, :], cell, halves)
+        part = slice(inner + index * WIDE, inner + index * WIDE + WIDE)
+        own = unsort(octant, oct_ref[index]) + sum_ref[index]
+        own += unsort(own_ref[part, :], picked(rest_ref, index, 0.0, WIDE))
+        own = (own[0:8] + own[8:16] + own[16:24]) * size_ref[index][1:2]
+        their = their_ref[index]
+        their = their[0:8] + their[8:16] + their[16:24]
+        active = side_ref[index, 5:6, :]
+        push = spot * own[3:4] - own[0:3]
+        heat = fields[4:7] * push - spot * own[4:7]
+        heat = jnp.sum(heat, axis=0, keepdims=True) + own[7:8]
+        push = push + spot * their[3:4] - their[0:3]
+        push_ref[cell] = jnp.concatenate([push, active], axis=0)
+        heat_ref[cell[0], cell[1], cell[2] : cell[2] + 1, :] = active * heat
+
+
 def main_kernel(
     src_ref,
     len_ref,
@@ -257,25 +446,23 @@
     early_ref,
     second_ref,
     rho_ref,
-    push_ref,
-    heat_ref,
     inner_ref,
     low_ref,
     high_ref,
-    dens_ref,
-    root_ref,
-    flat_ref,
-    col_ref,
     size_ref,
     left_ref,
     feat_ref,
     oct_ref,
     rest_ref,
+    own_ref,
+    sum_ref,
+    dens_ref,
+    root_ref,
+    flat_ref,
+    col_ref,
     far_ref,
     close_ref,
-    own_ref,
     their_ref,
-    sum_ref,
     count_ref,
     *,
     sizes,
@@ -294,15 +481,11 @@
     for x, y, z in cells_of(sizes):
         fields = src_ref[x, y, z]
         spot, square = place(fields, origin_of((x, y, z), sizes))
-        mass = fields[3:4]
         line = x * ny + y
         part = slice(z * 128, (z + 1) * 128)
         density_tables(dens_ref, root_ref, line, z, fields, spot, square)
         flat_ref[line, :, part] = source_rows(spot, square, 1.0).astype(jnp.bfloat16)
-        moving = jnp.sum(fields[4:7] * spot[0:3], axis=0, keepdims=True)
-        basis = jnp.where(row < 3, spot, jnp.where(row == 3, 1.0, fields))
-        basis = jnp.where(row == 7, moving, basis) * mass
-        cols = jnp.concatenate(split3(basis), axis=0).T.astype(jnp.bfloat16)
+        cols = force_columns(fields, spot)
         col_ref[line, z * 256 : z * 256 + 128, :] = cols
         col_ref[line, z * 256 + 128 : z * 256 + 256, :] = cols
 
@@ -333,21 +516,6 @@
 
     lax.fori_loop(0, cx, first_pass, 0)
 
-    def cell_runs(cell):
-        x, y, z = cell
-        return [
-            (((2 * x + bx) * halves[1] + 2 * y + by) * halves[2] + 2 * z) * 16
-            for bx in range(2)
-            for by in range(2)
-        ]
-
-    def scatter_rows(ref, cell, value):
-        for k, start in enumerate(cell_runs(cell)):
-            ref[start : start + 32, :] = value[k * 32 : (k + 1) * 32]
-
-    def gather_rows(value_of, cell):
-        return jnp.concatenate([value_of(start) for start in cell_runs(cell)], axis=0)
-
     def choose(index, fields, length):
         side = side_ref[index]
         reach = jnp.where(side > 0.0, length - fields, fields + length - 1.0)
@@ -361,48 +529,25 @@
         oct_ref[index] = jnp.where(slot_of == slot, 1.0, 0.0).astype(jnp.bfloat16)
         rest_ref[index] = jnp.broadcast_to(order, (8, 128))
 
-    def picked(index, first, count):
-        order = rest_ref[index][0:1] - first
-        slots = lax.broadcasted_iota(jnp.int32, (count, 128), 0).astype(jnp.float32)
-        return jnp.where(slots == order, 1.0, 0.0)
-
     def set_rows(index, cell, fields, spot, square, length, weight):
         inverse = 1.0 / length
         choose(index, fields, length)
         count = 16 if weight is None else WIDE
-        rest = picked(index, 0.0, count).astype(jnp.bfloat16)
+        rest = picked(rest_ref, index, 0.0, count).astype(jnp.bfloat16)
         left = target_rows(spot, square, inverse * inverse).astype(jnp.bfloat16)
         chosen = oct_ref[index]
-        scatter_rows(left_ref, cell, product_nt(chosen, left).astype(jnp.bfloat16))
+        scatter_rows(left_ref, cell, halves, product_nt(chosen, left).astype(jnp.bfloat16))
         part = slice(inner + index * WIDE, inner + index * WIDE + count)
         left_ref[part, :] = product_nt(rest, left).astype(jnp.bfloat16)
         if weight is not None:
             feat = jnp.concatenate(split3(weight), axis=0).astype(jnp.bfloat16)
-            scatter_rows(feat_ref, cell, product_nt(chosen, feat).astype(jnp.bfloat16))
+            scatter_rows(feat_ref, cell, halves, product_nt(chosen, feat).astype(jnp.bfloat16))
             feat_ref[part, :] = product_nt(rest, feat).astype(jnp.bfloat16)
-
-    def source_runs(x, y, z, count):
-        ranges = [halves_of(s, n) for s, n in zip((x, y, z), local)]
-        runs = runs_of(ranges, halves)
-        ranges = [near_of(s, n) for s, n in zip((x, y, z), local)]
-        for start, size in runs_of(ranges, local):
-            for first in range(start // 16, (start + size) // 16):
-                runs.append((inner + first * WIDE, count))
-        return runs
-
-    def rows_of(ref, runs):
-        return jnp.concatenate([ref[start : start + size, :] for start, size in runs], axis=0)
-
-    def add_rows(ref, runs, value):
-        at = 0
-        for start, size in runs:
-            ref[start : start + size, :] += value[at : at + size]
-            at += size
 
     def unsorted_column(index, octant, rest):
         total = jnp.sum(octant, axis=1, keepdims=True) * oct_ref[index].astype(jnp.float32)
         total = jnp.sum(total, axis=0, keepdims=True)
-        rest = jnp.sum(rest, axis=1, keepdims=True) * picked(index, 0.0, 16)
+        rest = jnp.sum(rest, axis=1, keepdims=True) * picked(rest_ref, index, 0.0, 16)
         return total + jnp.sum(rest, axis=0, keepdims=True)
 
     def extras(visit, first):
@@ -415,7 +560,7 @@
                 where = [v.astype(jnp.float32) + (1.0 - 0.5 * n) for v, n in zip((x, y, z), sizes)]
                 spot, square = place(fields, where)
                 inverse = 1.0 / size_ref[index][0:1]
-                rest = picked(index, chunk.astype(jnp.float32) * 16.0, 16)
+                rest = picked(rest_ref, index, chunk.astype(jnp.float32) * 16.0, 16)
                 left = target_rows(spot, square, inverse * inverse).astype(jnp.bfloat16)
                 left = product_nt(rest.astype(jnp.bfloat16), left).astype(jnp.bfloat16)
                 visit(index, (x, y, z), fields, spot, rest, left)
@@ -435,13 +580,6 @@
         extra = dense_sums(left, dens_ref, root_ref, spans)
         extra = jnp.sum(extra, axis=1, keepdims=True) * rest
         sum_ref[index, 0:8, :] += jnp.sum(extra, axis=0, keepdims=True)
-
-    def unsort(value, rest):
-        pieces = split3(value)
-        rest = rest.astype(jnp.bfloat16)
-        total = product_tn(pieces[0].astype(jnp.bfloat16), rest)
-        total += product_tn(pieces[1].astype(jnp.bfloat16), rest)
-        return total + product_tn(pieces[2].astype(jnp.bfloat16), rest)
 
     def extra_force(index, cell, fields, spot, rest, left):
         x, y, z = cell
@@ -473,7 +611,7 @@
     far_ref[...] = jnp.zeros_like(far_ref)
     close_ref[...] = jnp.zeros_like(close_ref)
     for x, y, z in cells_of(sizes):
-        runs = source_runs(x, y, z, 16)
+        runs = source_runs((x, y, z), local, 16)
         line = x * ny + y
         part = slice(z * 128, (z + 1) * 128)
         left = rows_of(left_ref, runs)
@@ -487,6 +625,7 @@
         octant = gather_rows(
             lambda start: 2.0 * far_ref[start : start + 32, :] - close_ref[start : start + 32, :],
             cell,
+            halves,
         )
         total = unsorted_column(index, octant, 2.0 * far_ref[part, :] - close_ref[part, :])
         sum_ref[index, 0:8, :] = jnp.broadcast_to(total, (8, 128))
@@ -505,47 +644,28 @@
 
     own_ref[...] = jnp.zeros_like(own_ref)
 
-    def slopes(x, y, z):
-        runs = source_runs(x, y, z, WIDE)
-        line = x * ny + y
-        part = slice(z * 128, (z + 1) * 128)
-        high, low = profile(product(rows_of(left_ref, runs), flat_ref[line, :, part]))
-        return line, z, runs, high, low
-
-    def sums(line, z, runs, high, low):
-        part = slice(z * 128, (z + 1) * 128)
-        cols = col_ref[line, z * 256 : (z + 1) * 256, :]
-        add_rows(own_ref, runs, product(jnp.concatenate([high, low], axis=1), cols))
-        feat = rows_of(feat_ref, runs)
-        their_ref[line, :, part] = product_tn(feat, high) + product_tn(feat, low)
-
-    waiting = None
-    for source in cells_of(sizes):
-        ready = slopes(*source)
-        if waiting is not None:
-            sums(*waiting)
-        waiting = ready
-    sums(*waiting)
-
-    for index, cell in enumerate(cells):
-        octant = gather_rows(lambda start: own_ref[start : start + 32, :], cell)
-        part = slice(inner + index * WIDE, inner + index * WIDE + WIDE)
-        own = unsort(octant, oct_ref[index]) + unsort(own_ref[part, :], picked(index, 0.0, WIDE))
-        sum_ref[index] = own
+    sum_ref[...] = jnp.zeros_like(sum_ref)
+    their_ref[...] = jnp.zeros_like(their_ref)
+
+    def part_of(source):
+        x, y, z = source
+        return x * ny + y, slice(z * 128, (z + 1) * 128)
+
+    def put(source, value):
+        line, part = part_of(source)
+        their_ref[line, :, part] = value
+
+    def flat_of(source):
+        line, part = part_of(source)
+        return flat_ref[line, :, part]
+
+    def cols_of(source):
+        x, y, z = source
+        return col_ref[x * ny + y, z * 256 : (z + 1) * 256, :]
+
+    outer = [cell for cell in cells_of(sizes) if cell[2] in (0, nz - 1)]
+    force_sums(outer, left_ref, feat_ref, own_ref, flat_of, cols_of, put, local)
     extras(extra_force, WIDE // 16)
-    for index, cell in enumerate(cells):
-        x, y, z = cell
-        fields, origin = placed[index]
-        spot, square = place(fields, origin)
-        own = sum_ref[index]
-        own = (own[0:8] + own[8:16] + own[16:24]) * size_ref[index][1:2]
-        active = side_ref[index, 5:6, :]
-        spot = spot[0:3]
-        push = spot * own[3:4] - own[0:3]
-        heat = fields[4:7] * push - spot * own[4:7]
-        heat = jnp.sum(heat, axis=0, keepdims=True) + own[7:8]
-        push_ref[x, y, z] = jnp.concatenate([push, active], axis=0)
-        heat_ref[x, y, z : z + 1, :] = active * heat
 
     for x, y, z in cells_of(sizes):
         spot, square = place(src_ref[x, y, z], origin_of((x, y, z), sizes))
@@ -583,19 +703,20 @@
     return lax.slice_in_dim(block, start, stop, axis=dim)
 
 
-def fold(block, low, high):
+def fold(block, low, high, edges):
     for dim in (2, 1, 0):
         axis = AXES[dim]
         if dim < 2:
             last = block.shape[dim] - 1
-            low, high = take(block, dim, 0, 1), take(block, dim, last, last + 1)
+            low = take(block, dim, 0, 1) + edges[dim][0]
+            high = take(block, dim, last, last + 1) + edges[dim][1]
             block = take(block, dim, 1, last)
         if lax.axis_size(axis) == 2:
-            both = lax.ppermute(jnp.concatenate([high, low], axis=dim), axis, ring(axis, 1))
+            both = move(jnp.concatenate([high, low], axis=dim), axis, 1)
             to_first, to_last = take(both, dim, 0, 1), take(both, dim, 1, 2)
         else:
-            to_last = lax.ppermute(low, axis, ring(axis, -1))
-            to_first = lax.ppermute(high, axis, ring(axis, 1))
+            to_last = move(low, axis, -1)
+            to_first = move(high, axis, 1)
         count = block.shape[dim]
         if count == 1:
             block = block + to_first + to_last
@@ -648,37 +769,66 @@
     padded = halo(tall, (2,))
     lines = nx * ny
     rows = ncell * (128 + WIDE)
-    density, push, heat, spread, low, high = pl.pallas_call(
+    density, inner, low, high, *kept = pl.pallas_call(
         functools.partial(main_kernel, sizes=sizes),
         out_shape=(
-            jax.ShapeDtypeStruct(masses.shape, f32),
-            jax.ShapeDtypeStruct(local + (4, 128), f32),
             jax.ShapeDtypeStruct(masses.shape, f32),
             jax.ShapeDtypeStruct((nx, ny, local[2], 4, 128), f32),
             jax.ShapeDtypeStruct((nx, ny, 1, 4, 128), f32),
             jax.ShapeDtypeStruct((nx, ny, 1, 4, 128), f32),
+            jax.ShapeDtypeStruct((ncell, 8, 128), f32),
+            jax.ShapeDtypeStruct((rows, 48), bf16),
+            jax.ShapeDtypeStruct((rows, 24), bf16),
+            jax.ShapeDtypeStruct((ncell, 128, 128), bf16),
+            jax.ShapeDtypeStruct((ncell, 8, 128), f32),
+            jax.ShapeDtypeStruct((rows, 24), f32),
+            jax.ShapeDtypeStruct((ncell, 24, 128), f32),
         ),
         scratch_shapes=[
             pltpu.VMEM((lines, 48, nz * 128), bf16),
             pltpu.VMEM((lines, 8, nz * 128), f32),
             pltpu.VMEM((lines, 48, nz * 128), bf16),
             pltpu.VMEM((lines, nz * 256, 24), bf16),
-            pltpu.VMEM((ncell, 8, 128), f32),
-            pltpu.VMEM((rows, 48), bf16),
-            pltpu.VMEM((rows, 24), bf16),
-            pltpu.VMEM((ncell, 128, 128), bf16),
-            pltpu.VMEM((ncell, 8, 128), f32),
             pltpu.VMEM((rows, 128), f32),
             pltpu.VMEM((rows, 128), f32),
-            pltpu.VMEM((rows, 24), f32),
             pltpu.VMEM((lines, 24, nz * 128), f32),
-            pltpu.VMEM((ncell, 24, 128), f32),
             pltpu.SMEM((ncell,), jnp.int32),
         ],
         compiler_params=pltpu.CompilerParams(vmem_limit_bytes=VMEM_LIMIT),
         name="main",
     )(padded, smoothing, side, early, second)
-    total = -(push[..., 0:3, :] + fold(spread, low, high)[..., 0:3, :]) * push[..., 3:4, :]
+
+    def edge(dim):
+        shape = [n if k < dim else n - 2 for k, n in enumerate(sizes)]
+        shape[dim] = 1
+        count = 2 * shape[0] * shape[1] * shape[2]
+        side_shape = jax.ShapeDtypeStruct(tuple(shape) + (4, 128), f32)
+        return pl.pallas_call(
+            functools.partial(edge_kernel, sizes=sizes, dim=dim),
+            out_shape=(jax.ShapeDtypeStruct((rows, 24), f32), side_shape, side_shape),
+            scratch_shapes=[pltpu.VMEM((count, 48, 128), bf16), pltpu.VMEM((count, 256, 24), bf16)],
+            compiler_params=pltpu.CompilerParams(vmem_limit_bytes=VMEM_LIMIT),
+        )(padded, kept[1], kept[2])
+
+    tall_own, *tall_edges = edge(1)
+    wide_own, *wide_edges = edge(0)
+    push, heat = pl.pallas_call(
+        functools.partial(rest_kernel, sizes=sizes),
+        out_shape=(
+            jax.ShapeDtypeStruct(local + (4, 128), f32),
+            jax.ShapeDtypeStruct(masses.shape, f32),
+        ),
+        scratch_shapes=[
+            pltpu.VMEM((ncell, 48, 128), bf16),
+            pltpu.VMEM((ncell, 256, 24), bf16),
+            pltpu.VMEM((rows, 24), f32),
+            pltpu.VMEM((ncell, 24, 128), f32),
+        ],
+        compiler_params=pltpu.CompilerParams(vmem_limit_bytes=VMEM_LIMIT),
+        name="rest",
+    )(static, side, *kept, wide_own, tall_own)
+    edges = (wide_edges, tall_edges)
+    total = -(push[..., 0:3, :] + fold(inner, low, high, edges)[..., 0:3, :]) * push[..., 3:4, :]
     return (density, jnp.moveaxis(total, 3, 0), heat)
 
 

time: 78.2 us -> 74.8 us (0.957)
  starting transfers between devices: 29 us -> 24.3 us
  Pallas kernels: 31.4 us -> 33.4 us
  waiting for transfers between devices: 14.4 us -> 13.6 us
    ppermute x5 -> x0, starting transfers between devices: 19.9 us -> none  [the longest x2 17 us: fold(): to_last = lax.ppermute(low, axis, ring(axis, -1))]
    ppermute x5 -> x10, starting transfers between devices: 9.06 us -> 24.3 us  [move(): return lax.ppermute(block, axis, ring(axis, step))]
    ppermute x5 -> x0, waiting for transfers between devices: 10.4 us -> none  [the longest x2 5.69 us: fold(): to_first = lax.ppermute(high, axis, ring(axis, 1))]
    ppermute x5 -> x10, waiting for transfers between devices: 4.07 us -> 13.6 us  [move(): return lax.ppermute(block, axis, ring(axis, step))]
    pallas_call x0 -> x3, Pallas kernels: none -> 6.85 us  [the longest x1 3.49 us: body(): pl.pallas_call(functools.partial(rest_kernel, sizes=sizes), out_shape=(ja...]
    pallas_call x1, Pallas kernels: 22.4 us -> 17.5 us  [body(): pl.pallas_call(functools.partial(main_kernel, sizes=sizes), out_shape=(ja...]
  transfers between devices with their start and end apart: 10 -> 10, of which waited for: 8 -> 6; matrix products, arithmetic and copies ran while one was open for 0% -> 0% of each run, Pallas kernels for 12% -> 21%
where the time goes in v3:
time: 74.8 us; the launch traced here: 74.4 us
  Pallas kernels  33.4 us (45%)
  starting transfers between devices  24.3 us (32%)
  waiting for transfers between devices  13.6 us (18%)
  local copies, waits for them, and re-layouts  2.22 us (3%)
  between operations  0.81 us (1%)
    ppermute x10, starting transfers between devices, move(): return lax.ppermute(block, axis, ring(axis, step))  24.3 us
    pallas_call x1, Pallas kernels, body(): pl.pallas_call(functools.partial(main_kernel, sizes=sizes), out_shape=(ja...  17.5 us
    ppermute x10, waiting for transfers between devices, move(): return lax.ppermute(block, axis, ring(axis, step))  13.6 us
    pallas_call x2, Pallas kernels, begin(): pl.pallas_call(functools.partial(early_kernel, sizes=sizes, crossing=cros...  6.07 us
    pallas_call x1, Pallas kernels, body(): pl.pallas_call(functools.partial(rest_kernel, sizes=sizes), out_shape=(ja...  3.49 us
    pallas_call x2, Pallas kernels, edge(): pl.pallas_call(functools.partial(edge_kernel, sizes=sizes, dim=dim), out_...  3.37 us
    pallas_call x1, Pallas kernels, body(): pl.pallas_call(functools.partial(sort_kernel, local=local), out_shape=jax...  2.95 us
  transfers between devices with their start and end apart: 10, of which 6 were waited for; matrix products, arithmetic and copies ran while one was open for 0% of the time, Pallas kernels for 21%

profile of v3, /device:TPU:0, one launch (start us, length us, event | category | flops | bytes accessed | tf_op | source)
XLA Modules:
  0.0 74.4 jit_solution(8356107928768645685)
XLA Ops:
  0.6 0.7 fusion.21
  1.4 0.0 copy-start.3
  1.4 0.7 copy-done.4
  2.1 0.0 copy-done.3
  2.1 0.1 stack.11.src_ref
  2.1 3.0 %collective-permute-start = (f32[2,2,2,8,128]{4,3,2,1,0:T(8,128)S(1)}, f32[2,2,2,8,128]{4,3,2,1,0:T(8,128)S(1)}, u32[]{:S(2)}, u32[]{:S(2)}) collective-permute-start(f32[2,2,2,8,128]{4,3,2,1,0:T(8,128)S(1)} %stack.11.src_ref), channel_id=1, source_target_pairs={{0,16},{16,0},{1,17},{17,1},{2,18},{18,2},{3,19},{19,3},{4,20},{20... | collective-permute-start | bytes 98312 | tf_op jit(solution)/shard_map/ppermute | solution.py:28
  5.2 1.9 %collective-permute-done = f32[2,2,2,8,128]{4,3,2,1,0:T(8,128)S(1)} collective-permute-done((f32[2,2,2,8,128]{4,3,2,1,0:T(8,128)S(1)}, f32[2,2,2,8,128]{4,3,2,1,0:T(8,128)S(1)}, u32[]{:S(2)}, u32[]{:S(2)}) %collective-permute-start) | collective-permute-done | bytes 32800 | tf_op jit(solution)/shard_map/ppermute | solution.py:28
  7.1 4.2 %collective-permute-start.2 = (f32[4,1,2,8,128]{4,3,2,1,0:T(8,128)S(1)}, f32[4,1,2,8,128]{4,3,2,1,0:T(8,128)S(1)}, u32[]{:S(2)}, u32[]{:S(2)}) collective-permute-start(f32[4,1,2,8,128]{4,3,2,1,0:T(8,128)S(1)} %get-tuple-element.53), channel_id=1, source_target_pairs={{0,12},{4,0},{8,4},{12,8},{1,13},{5,1},{9,5},{13,9},{2,14},{6,2},{... | collective-permute-start | bytes 98312 | tf_op jit(solution)/shard_map/ppermute | solution.py:28
  11.3 0.0 collective-permute-start.1
  11.3 1.6 %collective-permute-done.2 = f32[4,1,2,8,128]{4,3,2,1,0:T(8,128)S(1)} collective-permute-done((f32[4,1,2,8,128]{4,3,2,1,0:T(8,128)S(1)}, f32[4,1,2,8,128]{4,3,2,1,0:T(8,128)S(1)}, u32[]{:S(2)}, u32[]{:S(2)}) %collective-permute-start.2) | collective-permute-done | bytes 32800 | tf_op jit(solution)/shard_map/ppermute | solution.py:28
  12.9 4.1 %collective-permute-done.1 = f32[4,1,2,8,128]{4,3,2,1,0:T(8,128)S(1)} collective-permute-done((f32[4,1,2,8,128]{4,3,2,1,0:T(8,128)S(1)}, f32[4,1,2,8,128]{4,3,2,1,0:T(8,128)S(1)}, u32[]{:S(2)}, u32[]{:S(2)}) %collective-permute-start.1) | collective-permute-done | bytes 32800 | tf_op jit(solution)/shard_map/ppermute | solution.py:28
  17.0 0.0 copy-start.1
  17.0 0.1 collective-permute-start.4
  17.1 0.0 copy-start
  17.1 0.5 collective-permute-start.3
  17.6 0.1 copy-done.1
  17.7 2.9 %sort.1.side_ref = f32[8,8,128]{2,1,0:T(8,128)S(1)} custom-call(f32[2,2,2,8,128]{4,3,2,1,0:T(8,128)S(1)} %stack.11.src_ref, s32[2,2,2,128]{3,2,1,0:T(2,128)S(1)} %copy-done.1), custom_call_target="tpu_custom_call" | custom-call | tf_op jit(solution)/shard_map/sort/pallas_call | solution.py:746
  20.7 3.8 %shard_map.85.early_ref = f32[8,8,128]{2,1,0:T(8,128)S(1)} custom-call(f32[4,2,2,8,128]{4,3,2,1,0:T(8,128)S(1)} %pad_maximum_fusion.2.src_ref, f32[2,2,2,128]{3,2,1,0:T(2,128)S(1)} %copy-done), custom_call_target="tpu_custom_call" | custom-call | tf_op jit(solution)/shard_map/pallas_call | solution.py:756
  24.5 2.2 %shard_map.86.second_ref = f32[8,8,128]{2,1,0:T(8,128)S(1)} custom-call(f32[4,4,2,8,128]{4,3,2,1,0:T(8,128)S(1)} %pad_maximum_fusion.1.src_ref, f32[2,2,2,128]{3,2,1,0:T(2,128)S(1)} %copy-done), custom_call_target="tpu_custom_call" | custom-call | tf_op jit(solution)/shard_map/pallas_call | solution.py:756
  26.7 0.0 collective-permute-done.4
  26.8 17.5 %main.1 = (f32[2,2,2,128]{3,2,1,0:T(2,128)}, f32[4,4,2,4,128]{4,3,2,1,0:T(4,128)S(1)}, f32[4,4,1,4,128]{4,3,2,1,0:T(4,128)S(1)}, f32[4,4,1,4,128]{4,3,2,1,0:T(4,...) custom-call(f32[4,4,4,8,128]{4,3,2,1,0:T(8,128)S(1)} %pad_maximum_fu, ...), custom_call_target="tpu_custom_call" | custom-call | tf_op jit(solution)/shard_map/main/pallas_call | solution.py:772
  44.3 0.0 collective-permute-start.6
  44.3 2.1 %collective-permute-start.5 = (f32[4,4,1,4,128]{4,3,2,1,0:T(4,128)S(1)}, f32[4,4,1,4,128]{4,3,2,1,0:T(4,128)S(1)}, u32[]{:S(2)}, u32[]{:S(2)}) collective-permute-start(f32[4,4,1,4,128]{4,3,2,1,0:T(4,128)S(1)} %get-tuple-element.34), channel_id=1, source_target_pairs={{0,1},{1,2},{2,3},{3,0},{4,5},{5,6},{6,7},{7,4},{8,9},{9,10},{10,1... | collective-permute-start | bytes 98312 | tf_op jit(solution)/shard_map/ppermute | solution.py:28
  46.3 2.0 %shard_map.88 = (f32[1280,24]{1,0:T(8,128)S(1)}, f32[4,1,2,4,128]{4,3,2,1,0:T(4,128)S(1)}, f32[4,1,2,4,128]{4,3,2,1,0:T(4,128)S(1)}) custom-call(f32[4,4,4,8,128]{4,3,2,1,0:T(8,128)S(1)} %pad_maximum_fusion.src_ref, bf16[1280,48]{1,0:T(8,128)(2,1)S(1)} %get-tuple-element.24.left_ref, bf16[1280,24]{1,0:T(8,128)(2,1)S(1)} %get-tuple-element.25.feat_ref), custom_call_target="tpu_custom_call" | custom-call | tf_op jit(solution)/shard_map/pallas_call | solution.py:806
  48.3 1.8 %collective-permute-done.5 = f32[4,4,1,4,128]{4,3,2,1,0:T(4,128)S(1)} collective-permute-done((f32[4,4,1,4,128]{4,3,2,1,0:T(4,128)S(1)}, f32[4,4,1,4,128]{4,3,2,1,0:T(4,128)S(1)}, u32[]{:S(2)}, u32[]{:S(2)}) %collective-permute-start.5) | collective-permute-done | bytes 32800 | tf_op jit(solution)/shard_map/ppermute | solution.py:28
  50.2 12.5 %collective-permute-start.8 = (f32[4,1,2,4,128]{4,3,2,1,0:T(4,128)S(1)}, f32[4,1,2,4,128]{4,3,2,1,0:T(4,128)S(1)}, u32[]{:S(2)}, u32[]{:S(2)}) collective-permute-start(f32[4,1,2,4,128]{4,3,2,1,0:T(4,128)S(1)} %get-tuple-element.48), channel_id=1, source_target_pairs={{0,12},{4,0},{8,4},{12,8},{1,13},{5,1},{9,5},{13,9},{2,14},{6,2},{... | collective-permute-start | bytes 49160 | tf_op jit(solution)/shard_map/ppermute | solution.py:28
  62.6 1.4 %shard_map.87 = (f32[1280,24]{1,0:T(8,128)S(1)}, f32[1,2,2,4,128]{4,3,2,1,0:T(4,128)S(1)}, f32[1,2,2,4,128]{4,3,2,1,0:T(4,128)S(1)}) custom-call(f32[4,4,4,8,128]{4,3,2,1,0:T(8,128)S(1)} %pad_maximum_fusion.src_ref, bf16[1280,48]{1,0:T(8,128)(2,1)S(1)} %get-tuple-element.24.left_ref, bf16[1280,24]{1,0:T(8,128)(2,1)S(1)} %get-tuple-element.25.feat_ref), custom_call_target="tpu_custom_call" | custom-call | tf_op jit(solution)/shard_map/pallas_call | solution.py:806
  64.0 0.1 collective-permute-done.8
  64.1 4.1 %collective-permute-done.7 = f32[4,1,2,4,128]{4,3,2,1,0:T(4,128)S(1)} collective-permute-done((f32[4,1,2,4,128]{4,3,2,1,0:T(4,128)S(1)}, f32[4,1,2,4,128]{4,3,2,1,0:T(4,128)S(1)}, u32[]{:S(2)}, u32[]{:S(2)}) %collective-permute-start.7) | collective-permute-done | bytes 16416 | tf_op jit(solution)/shard_map/ppermute | solution.py:28
  68.2 2.0 %collective-permute-start.9 = (f32[2,2,2,4,128]{4,3,2,1,0:T(4,128)S(1)}, f32[2,2,2,4,128]{4,3,2,1,0:T(4,128)S(1)}, u32[]{:S(2)}, u32[]{:S(2)}) collective-permute-start(f32[2,2,2,4,128]{4,3,2,1,0:T(4,128)S(1)} %pad_maximum_fusion.5), channel_id=1, source_target_pairs={{0,16},{16,0},{1,17},{17,1},{2,18},{18,2},{3,19},{19,3},{4,20},{20... | collective-permute-start | bytes 49160 | tf_op jit(solution)/shard_map/ppermute | solution.py:28
  70.3 3.5 %rest.1 = (f32[2,2,2,4,128]{4,3,2,1,0:T(4,128)S(1)}, f32[2,2,2,128]{3,2,1,0:T(2,128)}) custom-call(f32[2,2,2,8,128]{4,3,2,1,0:T(8,128)S(1)} %stack.11.src_ref, f32[8,8,128]{2,1,0:T(8,128)S(1)} %sort.1.side_ref, f32[8,8,128]{2,1,0:T(8,128)S(1)} %get-tuple-element.23.size_ref, bf16[1280,48]{1,0:T(8,128)(2,1)S(1)} %get-tuple-element.24.left_ref, ...), custom_call_target="tpu_custom_call" | custom-call | tf_op jit(solution)/shard_map/rest/pallas_call | solution.py:815
  73.8 0.6 copy.9
  (23 shorter events, 0.2 us)
Async XLA Ops:
  0.6 0.7 copy-start.2
  1.4 0.7 copy-start.4
  1.4 0.7 copy-start.3
  2.1 4.9 %collective-permute-start = (f32[2,2,2,8,128]{4,3,2,1,0:T(8,128)S(1)}, f32[2,2,2,8,128]{4,3,2,1,0:T(8,128)S(1)}, u32[]{:S(2)}, u32[]{:S(2)}) collective-permute-start(f32[2,2,2,8,128]{4,3,2,1,0:T(8,128)S(1)} %stack.11.src_ref), channel_id=1, source_target_pairs={{0,16},{16,0},{1,17},{17,1},{2,18},{18,2},{3,19},{19,3},{4,20},{20... | collective-permute-start | bytes 98312 | tf_op jit(solution)/shard_map/ppermute | solution.py:28
  7.1 5.8 %collective-permute-start.2 = (f32[4,1,2,8,128]{4,3,2,1,0:T(8,128)S(1)}, f32[4,1,2,8,128]{4,3,2,1,0:T(8,128)S(1)}, u32[]{:S(2)}, u32[]{:S(2)}) collective-permute-start(f32[4,1,2,8,128]{4,3,2,1,0:T(8,128)S(1)} %get-tuple-element.53), channel_id=1, source_target_pairs={{0,12},{4,0},{8,4},{12,8},{1,13},{5,1},{9,5},{13,9},{2,14},{6,2},{... | collective-permute-start | bytes 98312 | tf_op jit(solution)/shard_map/ppermute | solution.py:28
  11.3 5.7 %collective-permute-start.1 = (f32[4,1,2,8,128]{4,3,2,1,0:T(8,128)S(1)}, f32[4,1,2,8,128]{4,3,2,1,0:T(8,128)S(1)}, u32[]{:S(2)}, u32[]{:S(2)}) collective-permute-start(f32[4,1,2,8,128]{4,3,2,1,0:T(8,128)S(1)} %get-tuple-element.52), channel_id=1, source_target_pairs={{0,4},{4,8},{8,12},{12,0},{1,5},{5,9},{9,13},{13,1},{2,6},{6,10},{... | collective-permute-start | bytes 98312 | tf_op jit(solution)/shard_map/ppermute | solution.py:28
  17.0 0.7 copy-start.1
  17.0 9.7 %collective-permute-start.4 = (f32[4,4,1,8,128]{4,3,2,1,0:T(8,128)S(1)}, f32[4,4,1,8,128]{4,3,2,1,0:T(8,128)S(1)}, u32[]{:S(2)}, u32[]{:S(2)}) collective-permute-start(f32[4,4,1,8,128]{4,3,2,1,0:T(8,128)S(1)} %get-tuple-element.45), channel_id=1, source_target_pairs={{0,3},{1,0},{2,1},{3,2},{4,7},{5,4},{6,5},{7,6},{8,11},{9,8},{10,9... | collective-permute-start | bytes 196616 | tf_op jit(solution)/shard_map/ppermute | solution.py:28
  17.1 3.5 %copy-start = (f32[2,2,2,128]{3,2,1,0:T(2,128)S(1)}, f32[2,2,2,128]{3,2,1,0:T(2,128)}, u32[]{:S(2)}) copy-start(f32[2,2,2,128]{3,2,1,0:T(2,128)} %len_ref.5) | copy-start | bytes 12292
  17.1 9.6 %collective-permute-start.3 = (f32[4,4,1,8,128]{4,3,2,1,0:T(8,128)S(1)}, f32[4,4,1,8,128]{4,3,2,1,0:T(8,128)S(1)}, u32[]{:S(2)}, u32[]{:S(2)}) collective-permute-start(f32[4,4,1,8,128]{4,3,2,1,0:T(8,128)S(1)} %get-tuple-element.44), channel_id=1, source_target_pairs={{0,1},{1,2},{2,3},{3,0},{4,5},{5,6},{6,7},{7,4},{8,9},{9,10},{10,1... | collective-permute-start | bytes 196616 | tf_op jit(solution)/shard_map/ppermute | solution.py:28
  44.3 4.1 %collective-permute-start.6 = (f32[4,4,1,4,128]{4,3,2,1,0:T(4,128)S(1)}, f32[4,4,1,4,128]{4,3,2,1,0:T(4,128)S(1)}, u32[]{:S(2)}, u32[]{:S(2)}) collective-permute-start(f32[4,4,1,4,128]{4,3,2,1,0:T(4,128)S(1)} %get-tuple-element.35), channel_id=1, source_target_pairs={{0,3},{1,0},{2,1},{3,2},{4,7},{5,4},{6,5},{7,6},{8,11},{9,8},{10,9... | collective-permute-start | bytes 98312 | tf_op jit(solution)/shard_map/ppermute | solution.py:28
  44.3 5.9 %collective-permute-start.5 = (f32[4,4,1,4,128]{4,3,2,1,0:T(4,128)S(1)}, f32[4,4,1,4,128]{4,3,2,1,0:T(4,128)S(1)}, u32[]{:S(2)}, u32[]{:S(2)}) collective-permute-start(f32[4,4,1,4,128]{4,3,2,1,0:T(4,128)S(1)} %get-tuple-element.34), channel_id=1, source_target_pairs={{0,1},{1,2},{2,3},{3,0},{4,5},{5,6},{6,7},{7,4},{8,9},{9,10},{10,1... | collective-permute-start | bytes 98312 | tf_op jit(solution)/shard_map/ppermute | solution.py:28
  50.2 13.9 %collective-permute-start.8 = (f32[4,1,2,4,128]{4,3,2,1,0:T(4,128)S(1)}, f32[4,1,2,4,128]{4,3,2,1,0:T(4,128)S(1)}, u32[]{:S(2)}, u32[]{:S(2)}) collective-permute-start(f32[4,1,2,4,128]{4,3,2,1,0:T(4,128)S(1)} %get-tuple-element.48), channel_id=1, source_target_pairs={{0,12},{4,0},{8,4},{12,8},{1,13},{5,1},{9,5},{13,9},{2,14},{6,2},{... | collective-permute-start | bytes 49160 | tf_op jit(solution)/shard_map/ppermute | solution.py:28
  62.6 5.5 %collective-permute-start.7 = (f32[4,1,2,4,128]{4,3,2,1,0:T(4,128)S(1)}, f32[4,1,2,4,128]{4,3,2,1,0:T(4,128)S(1)}, u32[]{:S(2)}, u32[]{:S(2)}) collective-permute-start(f32[4,1,2,4,128]{4,3,2,1,0:T(4,128)S(1)} %get-tuple-element.49), channel_id=1, source_target_pairs={{0,4},{4,8},{8,12},{12,0},{1,5},{5,9},{9,13},{13,1},{2,6},{6,10},{... | collective-permute-start | bytes 49160 | tf_op jit(solution)/shard_map/ppermute | solution.py:28
  68.2 5.5 %collective-permute-start.9 = (f32[2,2,2,4,128]{4,3,2,1,0:T(4,128)S(1)}, f32[2,2,2,4,128]{4,3,2,1,0:T(4,128)S(1)}, u32[]{:S(2)}, u32[]{:S(2)}) collective-permute-start(f32[2,2,2,4,128]{4,3,2,1,0:T(4,128)S(1)} %pad_maximum_fusion.5), channel_id=1, source_target_pairs={{0,16},{16,0},{1,17},{17,1},{2,18},{18,2},{3,19},{19,3},{4,20},{20... | collective-permute-start | bytes 49160 | tf_op jit(solution)/shard_map/ppermute | solution.py:28

commit v4 on v3

--- a/solution.py
+++ b/solution.py
@@ -332,45 +332,6 @@
     return all(0 < c <= n for c, n in zip(cell, local))
 
 
-def edge_kernel(
-    src_ref, left_ref, feat_ref, own_ref, low_ref, high_ref, flat_ref, col_ref, *, sizes, dim
-):
-    local = tuple(n - 2 for n in sizes)
-    ends = (0, sizes[dim] - 1)
-    numbers = {}
-    for cell in cells_of(sizes):
-        if cell[dim] in ends and all(0 < cell[k] <= local[k] for k in range(dim + 1, 3)):
-            if dim == 1 or is_local(cell[1:], local[1:]):
-                numbers[cell] = len(numbers)
-    for cell, index in numbers.items():
-        fields = src_ref[cell]
-        spot, square = place(fields, origin_of(cell, sizes))
-        flat_ref[index] = source_rows(spot, square, 1.0).astype(jnp.bfloat16)
-        cols = force_columns(fields, spot)
-        col_ref[index, 0:128, :] = cols
-        col_ref[index, 128:256, :] = cols
-    own_ref[...] = jnp.zeros_like(own_ref)
-
-    def put(source, value):
-        spot, _ = place(src_ref[source], origin_of(source, sizes))
-        their = value[0:8] + value[8:16] + value[16:24]
-        at = [c if k < dim else c - 1 for k, c in enumerate(source)]
-        at[dim] = 0
-        ref = low_ref if source[dim] == 0 else high_ref
-        ref[tuple(at)] = (spot * their[3:4] - their)[0:4]
-
-    force_sums(
-        list(numbers),
-        left_ref,
-        feat_ref,
-        own_ref,
-        lambda source: flat_ref[numbers[source]],
-        lambda source: col_ref[numbers[source]],
-        put,
-        local,
-    )
-
-
 def rest_kernel(
     src_ref,
     side_ref,
@@ -381,8 +342,6 @@
     rest_ref,
     part_ref,
     sum_ref,
-    wide_ref,
-    tall_ref,
     push_ref,
     heat_ref,
     flat_ref,
@@ -406,7 +365,7 @@
         col_ref[index, 0:128, :] = cols
         col_ref[index, 128:256, :] = cols
         places.append((fields, spot[0:3]))
-    own_ref[...] = part_ref[...] + wide_ref[...] + tall_ref[...]
+    own_ref[...] = part_ref[...]
 
     def put(source, value):
         their_ref[numbers[source]] = value
@@ -644,8 +603,10 @@
 
     own_ref[...] = jnp.zeros_like(own_ref)
 
-    sum_ref[...] = jnp.zeros_like(sum_ref)
-    their_ref[...] = jnp.zeros_like(their_ref)
+    for index, cell in enumerate(cells):
+        sum_ref[index] = jnp.zeros((24, 128), jnp.float32)
+        x, y, z = [c + 1 for c in cell]
+        their_ref[x * ny + y, :, z * 128 : (z + 1) * 128] = jnp.zeros((24, 128), jnp.float32)
 
     def part_of(source):
         x, y, z = source
@@ -663,7 +624,7 @@
         x, y, z = source
         return col_ref[x * ny + y, z * 256 : (z + 1) * 256, :]
 
-    outer = [cell for cell in cells_of(sizes) if cell[2] in (0, nz - 1)]
+    outer = [cell for cell in cells_of(sizes) if not is_local(cell, local)]
     force_sums(outer, left_ref, feat_ref, own_ref, flat_of, cols_of, put, local)
     extras(extra_force, WIDE // 16)
 
@@ -703,13 +664,12 @@
     return lax.slice_in_dim(block, start, stop, axis=dim)
 
 
-def fold(block, low, high, edges):
+def fold(block, low, high):
     for dim in (2, 1, 0):
         axis = AXES[dim]
         if dim < 2:
             last = block.shape[dim] - 1
-            low = take(block, dim, 0, 1) + edges[dim][0]
-            high = take(block, dim, last, last + 1) + edges[dim][1]
+            low, high = take(block, dim, 0, 1), take(block, dim, last, last + 1)
             block = take(block, dim, 1, last)
         if lax.axis_size(axis) == 2:
             both = move(jnp.concatenate([high, low], axis=dim), axis, 1)
@@ -797,21 +757,6 @@
         compiler_params=pltpu.CompilerParams(vmem_limit_bytes=VMEM_LIMIT),
         name="main",
     )(padded, smoothing, side, early, second)
-
-    def edge(dim):
-        shape = [n if k < dim else n - 2 for k, n in enumerate(sizes)]
-        shape[dim] = 1
-        count = 2 * shape[0] * shape[1] * shape[2]
-        side_shape = jax.ShapeDtypeStruct(tuple(shape) + (4, 128), f32)
-        return pl.pallas_call(
-            functools.partial(edge_kernel, sizes=sizes, dim=dim),
-            out_shape=(jax.ShapeDtypeStruct((rows, 24), f32), side_shape, side_shape),
-            scratch_shapes=[pltpu.VMEM((count, 48, 128), bf16), pltpu.VMEM((count, 256, 24), bf16)],
-            compiler_params=pltpu.CompilerParams(vmem_limit_bytes=VMEM_LIMIT),
-        )(padded, kept[1], kept[2])
-
-    tall_own, *tall_edges = edge(1)
-    wide_own, *wide_edges = edge(0)
     push, heat = pl.pallas_call(
         functools.partial(rest_kernel, sizes=sizes),
         out_shape=(
@@ -826,9 +771,8 @@
         ],
         compiler_params=pltpu.CompilerParams(vmem_limit_bytes=VMEM_LIMIT),
         name="rest",
-    )(static, side, *kept, wide_own, tall_own)
-    edges = (wide_edges, tall_edges)
-    total = -(push[..., 0:3, :] + fold(inner, low, high, edges)[..., 0:3, :]) * push[..., 3:4, :]
+    )(static, side, *kept)
+    total = -(push[..., 0:3, :] + fold(inner, low, high)[..., 0:3, :]) * push[..., 3:4, :]
     return (density, jnp.moveaxis(total, 3, 0), heat)
 
 

time: 74.8 us -> 78.3 us (1.047)
  starting transfers between devices: 24.3 us -> 29 us
  waiting for transfers between devices: 13.6 us -> 12.7 us
    ppermute x10, starting transfers between devices: 24.3 us -> 29 us  [move(): return lax.ppermute(block, axis, ring(axis, step))]
    pallas_call x2 -> x0, Pallas kernels: 3.37 us -> none  [edge(): pl.pallas_call(functools.partial(edge_kernel, sizes=sizes, dim=dim), out_...]
    pallas_call x1, Pallas kernels: 17.5 us -> 20.3 us  [body(): pl.pallas_call(functools.partial(main_kernel, sizes=sizes), out_shape=(ja...]
    ppermute x10, waiting for transfers between devices: 13.6 us -> 12.7 us  [move(): return lax.ppermute(block, axis, ring(axis, step))]
  transfers between devices with their start and end apart: 10 -> 10, of which waited for: 6 -> 7; matrix products, arithmetic and copies ran while one was open for 0% -> 0% of each run, Pallas kernels for 21% -> 16%
where the time goes in v4:
time: 78.3 us; the launch traced here: 77.5 us
  Pallas kernels  32.8 us (42%)
  starting transfers between devices  29 us (37%)
  waiting for transfers between devices  12.7 us (16%)
  local copies, waits for them, and re-layouts  2.13 us (3%)
  between operations  0.8 us (1%)
    ppermute x10, starting transfers between devices, move(): return lax.ppermute(block, axis, ring(axis, step))  29 us
    pallas_call x1, Pallas kernels, body(): pl.pallas_call(functools.partial(main_kernel, sizes=sizes), out_shape=(ja...  20.3 us
    ppermute x10, waiting for transfers between devices, move(): return lax.ppermute(block, axis, ring(axis, step))  12.7 us
    pallas_call x2, Pallas kernels, begin(): pl.pallas_call(functools.partial(early_kernel, sizes=sizes, crossing=cros...  6.07 us
    pallas_call x1, Pallas kernels, body(): pl.pallas_call(functools.partial(rest_kernel, sizes=sizes), out_shape=(ja...  3.49 us
    pallas_call x1, Pallas kernels, body(): pl.pallas_call(functools.partial(sort_kernel, local=local), out_shape=jax...  2.95 us
  transfers between devices with their start and end apart: 10, of which 7 were waited for; matrix products, arithmetic and copies ran while one was open for 0% of the time, Pallas kernels for 16%

profile of v4, /device:TPU:0, one launch (start us, length us, event | category | flops | bytes accessed | tf_op | source)
XLA Modules:
  0.0 77.5 jit_solution(7383122196330218337)
XLA Ops:
  0.6 0.7 fusion.17
  1.4 0.0 copy-start.3
  1.4 0.7 copy-done.4
  2.1 0.0 copy-done.3
  2.1 0.1 stack.11.src_ref
  2.1 3.0 %collective-permute-start = (f32[2,2,2,8,128]{4,3,2,1,0:T(8,128)S(1)}, f32[2,2,2,8,128]{4,3,2,1,0:T(8,128)S(1)}, u32[]{:S(2)}, u32[]{:S(2)}) collective-permute-start(f32[2,2,2,8,128]{4,3,2,1,0:T(8,128)S(1)} %stack.11.src_ref), channel_id=1, source_target_pairs={{0,16},{16,0},{1,17},{17,1},{2,18},{18,2},{3,19},{19,3},{4,20},{20... | collective-permute-start | bytes 98312 | tf_op jit(solution)/shard_map/ppermute | solution.py:28
  5.2 1.9 %collective-permute-done = f32[2,2,2,8,128]{4,3,2,1,0:T(8,128)S(1)} collective-permute-done((f32[2,2,2,8,128]{4,3,2,1,0:T(8,128)S(1)}, f32[2,2,2,8,128]{4,3,2,1,0:T(8,128)S(1)}, u32[]{:S(2)}, u32[]{:S(2)}) %collective-permute-start) | collective-permute-done | bytes 32800 | tf_op jit(solution)/shard_map/ppermute | solution.py:28
  7.1 2.2 %collective-permute-start.1 = (f32[4,1,2,8,128]{4,3,2,1,0:T(8,128)S(1)}, f32[4,1,2,8,128]{4,3,2,1,0:T(8,128)S(1)}, u32[]{:S(2)}, u32[]{:S(2)}) collective-permute-start(f32[4,1,2,8,128]{4,3,2,1,0:T(8,128)S(1)} %get-tuple-element.40), channel_id=1, source_target_pairs={{0,4},{4,8},{8,12},{12,0},{1,5},{5,9},{9,13},{13,1},{2,6},{6,10},{... | collective-permute-start | bytes 98312 | tf_op jit(solution)/shard_map/ppermute | solution.py:28
  9.2 2.1 %collective-permute-start.2 = (f32[4,1,2,8,128]{4,3,2,1,0:T(8,128)S(1)}, f32[4,1,2,8,128]{4,3,2,1,0:T(8,128)S(1)}, u32[]{:S(2)}, u32[]{:S(2)}) collective-permute-start(f32[4,1,2,8,128]{4,3,2,1,0:T(8,128)S(1)} %get-tuple-element.41), channel_id=1, source_target_pairs={{0,12},{4,0},{8,4},{12,8},{1,13},{5,1},{9,5},{13,9},{2,14},{6,2},{... | collective-permute-start | bytes 98312 | tf_op jit(solution)/shard_map/ppermute | solution.py:28
  11.3 1.9 %collective-permute-done.1 = f32[4,1,2,8,128]{4,3,2,1,0:T(8,128)S(1)} collective-permute-done((f32[4,1,2,8,128]{4,3,2,1,0:T(8,128)S(1)}, f32[4,1,2,8,128]{4,3,2,1,0:T(8,128)S(1)}, u32[]{:S(2)}, u32[]{:S(2)}) %collective-permute-start.1) | collective-permute-done | bytes 32800 | tf_op jit(solution)/shard_map/ppermute | solution.py:28
  13.3 0.2 collective-permute-done.2
  13.5 0.0 copy-start.1
  13.6 0.1 collective-permute-start.3
  13.6 0.0 copy-start
  13.6 1.7 %collective-permute-start.4 = (f32[4,4,1,8,128]{4,3,2,1,0:T(8,128)S(1)}, f32[4,4,1,8,128]{4,3,2,1,0:T(8,128)S(1)}, u32[]{:S(2)}, u32[]{:S(2)}) collective-permute-start(f32[4,4,1,8,128]{4,3,2,1,0:T(8,128)S(1)} %get-tuple-element.33), channel_id=1, source_target_pairs={{0,3},{1,0},{2,1},{3,2},{4,7},{5,4},{6,5},{7,6},{8,11},{9,8},{10,9... | collective-permute-start | bytes 196616 | tf_op jit(solution)/shard_map/ppermute | solution.py:28
  15.4 2.9 %sort.1.side_ref = f32[8,8,128]{2,1,0:T(8,128)S(1)} custom-call(f32[2,2,2,8,128]{4,3,2,1,0:T(8,128)S(1)} %stack.11.src_ref, s32[2,2,2,128]{3,2,1,0:T(2,128)S(1)} %copy-done.1), custom_call_target="tpu_custom_call" | custom-call | tf_op jit(solution)/shard_map/sort/pallas_call | solution.py:706
  18.3 3.8 %shard_map.85.early_ref = f32[8,8,128]{2,1,0:T(8,128)S(1)} custom-call(f32[4,2,2,8,128]{4,3,2,1,0:T(8,128)S(1)} %pad_maximum_fusion.2.src_ref, f32[2,2,2,128]{3,2,1,0:T(2,128)S(1)} %copy-done), custom_call_target="tpu_custom_call" | custom-call | tf_op jit(solution)/shard_map/pallas_call | solution.py:716
  22.2 2.2 %shard_map.86.second_ref = f32[8,8,128]{2,1,0:T(8,128)S(1)} custom-call(f32[4,4,2,8,128]{4,3,2,1,0:T(8,128)S(1)} %pad_maximum_fusion.1.src_ref, f32[2,2,2,128]{3,2,1,0:T(2,128)S(1)} %copy-done), custom_call_target="tpu_custom_call" | custom-call | tf_op jit(solution)/shard_map/pallas_call | solution.py:716
  24.4 0.0 collective-permute-done.3
  24.4 0.0 collective-permute-done.4
  24.5 20.3 %main.1 = (f32[2,2,2,128]{3,2,1,0:T(2,128)}, f32[4,4,2,4,128]{4,3,2,1,0:T(4,128)S(1)}, f32[4,4,1,4,128]{4,3,2,1,0:T(4,128)S(1)}, f32[4,4,1,4,128]{4,3,2,1,0:T(4,...) custom-call(f32[4,4,4,8,128]{4,3,2,1,0:T(8,128)S(1)} %pad_maximum_fu, ...), custom_call_target="tpu_custom_call" | custom-call | tf_op jit(solution)/shard_map/main/pallas_call | solution.py:732
  44.8 0.8 %collective-permute-start.5 = (f32[4,4,1,4,128]{4,3,2,1,0:T(4,128)S(1)}, f32[4,4,1,4,128]{4,3,2,1,0:T(4,128)S(1)}, u32[]{:S(2)}, u32[]{:S(2)}) collective-permute-start(f32[4,4,1,4,128]{4,3,2,1,0:T(4,128)S(1)} %get-tuple-element.26), channel_id=1, source_target_pairs={{0,1},{1,2},{2,3},{3,0},{4,5},{5,6},{6,7},{7,4},{8,9},{9,10},{10,1... | collective-permute-start | bytes 98312 | tf_op jit(solution)/shard_map/ppermute | solution.py:28
  45.6 0.9 %collective-permute-start.6 = (f32[4,4,1,4,128]{4,3,2,1,0:T(4,128)S(1)}, f32[4,4,1,4,128]{4,3,2,1,0:T(4,128)S(1)}, u32[]{:S(2)}, u32[]{:S(2)}) collective-permute-start(f32[4,4,1,4,128]{4,3,2,1,0:T(4,128)S(1)} %get-tuple-element.27), channel_id=1, source_target_pairs={{0,3},{1,0},{2,1},{3,2},{4,7},{5,4},{6,5},{7,6},{8,11},{9,8},{10,9... | collective-permute-start | bytes 98312 | tf_op jit(solution)/shard_map/ppermute | solution.py:28
  46.5 1.6 %collective-permute-done.5 = f32[4,4,1,4,128]{4,3,2,1,0:T(4,128)S(1)} collective-permute-done((f32[4,4,1,4,128]{4,3,2,1,0:T(4,128)S(1)}, f32[4,4,1,4,128]{4,3,2,1,0:T(4,128)S(1)}, u32[]{:S(2)}, u32[]{:S(2)}) %collective-permute-start.5) | collective-permute-done | bytes 32800 | tf_op jit(solution)/shard_map/ppermute | solution.py:28
  48.1 1.5 %collective-permute-done.6 = f32[4,4,1,4,128]{4,3,2,1,0:T(4,128)S(1)} collective-permute-done((f32[4,4,1,4,128]{4,3,2,1,0:T(4,128)S(1)}, f32[4,4,1,4,128]{4,3,2,1,0:T(4,128)S(1)}, u32[]{:S(2)}, u32[]{:S(2)}) %collective-permute-start.6) | collective-permute-done | bytes 32800 | tf_op jit(solution)/shard_map/ppermute | solution.py:28
  49.6 16.2 %collective-permute-start.8 = (f32[4,1,2,4,128]{4,3,2,1,0:T(4,128)S(1)}, f32[4,1,2,4,128]{4,3,2,1,0:T(4,128)S(1)}, u32[]{:S(2)}, u32[]{:S(2)}) collective-permute-start(f32[4,1,2,4,128]{4,3,2,1,0:T(4,128)S(1)} %get-tuple-element.36), channel_id=1, source_target_pairs={{0,12},{4,0},{8,4},{12,8},{1,13},{5,1},{9,5},{13,9},{2,14},{6,2},{... | collective-permute-start | bytes 49160 | tf_op jit(solution)/shard_map/ppermute | solution.py:28
  65.8 0.0 collective-permute-start.7
  65.8 1.4 %collective-permute-done.8 = f32[4,1,2,4,128]{4,3,2,1,0:T(4,128)S(1)} collective-permute-done((f32[4,1,2,4,128]{4,3,2,1,0:T(4,128)S(1)}, f32[4,1,2,4,128]{4,3,2,1,0:T(4,128)S(1)}, u32[]{:S(2)}, u32[]{:S(2)}) %collective-permute-start.8) | collective-permute-done | bytes 16416 | tf_op jit(solution)/shard_map/ppermute | solution.py:28
  67.2 4.1 %collective-permute-done.7 = f32[4,1,2,4,128]{4,3,2,1,0:T(4,128)S(1)} collective-permute-done((f32[4,1,2,4,128]{4,3,2,1,0:T(4,128)S(1)}, f32[4,1,2,4,128]{4,3,2,1,0:T(4,128)S(1)}, u32[]{:S(2)}, u32[]{:S(2)}) %collective-permute-start.7) | collective-permute-done | bytes 16416 | tf_op jit(solution)/shard_map/ppermute | solution.py:28
  71.3 2.0 %collective-permute-start.9 = (f32[2,2,2,4,128]{4,3,2,1,0:T(4,128)S(1)}, f32[2,2,2,4,128]{4,3,2,1,0:T(4,128)S(1)}, u32[]{:S(2)}, u32[]{:S(2)}) collective-permute-start(f32[2,2,2,4,128]{4,3,2,1,0:T(4,128)S(1)} %pad_maximum_fusion.5), channel_id=1, source_target_pairs={{0,16},{16,0},{1,17},{17,1},{2,18},{18,2},{3,19},{19,3},{4,20},{20... | collective-permute-start | bytes 49160 | tf_op jit(solution)/shard_map/ppermute | solution.py:28
  73.4 3.5 %rest.1 = (f32[2,2,2,4,128]{4,3,2,1,0:T(4,128)S(1)}, f32[2,2,2,128]{3,2,1,0:T(2,128)}) custom-call(f32[2,2,2,8,128]{4,3,2,1,0:T(8,128)S(1)} %stack.11.src_ref, f32[8,8,128]{2,1,0:T(8,128)S(1)} %sort.1.side_ref, f32[8,8,128]{2,1,0:T(8,128)S(1)} %get-tuple-element.17.size_ref, bf16[1280,48]{1,0:T(8,128)(2,1)S(1)} %get-tuple-element.18.left_ref, ...), custom_call_target="tpu_custom_call" | custom-call | tf_op jit(solution)/shard_map/rest/pallas_call | solution.py:760
  76.9 0.6 copy.9
  (21 shorter events, 0.2 us)
Async XLA Ops:
  0.6 0.7 copy-start.2
  1.4 0.7 copy-start.4
  1.4 0.7 copy-start.3
  2.1 4.9 %collective-permute-start = (f32[2,2,2,8,128]{4,3,2,1,0:T(8,128)S(1)}, f32[2,2,2,8,128]{4,3,2,1,0:T(8,128)S(1)}, u32[]{:S(2)}, u32[]{:S(2)}) collective-permute-start(f32[2,2,2,8,128]{4,3,2,1,0:T(8,128)S(1)} %stack.11.src_ref), channel_id=1, source_target_pairs={{0,16},{16,0},{1,17},{17,1},{2,18},{18,2},{3,19},{19,3},{4,20},{20... | collective-permute-start | bytes 98312 | tf_op jit(solution)/shard_map/ppermute | solution.py:28
  7.1 6.2 %collective-permute-start.1 = (f32[4,1,2,8,128]{4,3,2,1,0:T(8,128)S(1)}, f32[4,1,2,8,128]{4,3,2,1,0:T(8,128)S(1)}, u32[]{:S(2)}, u32[]{:S(2)}) collective-permute-start(f32[4,1,2,8,128]{4,3,2,1,0:T(8,128)S(1)} %get-tuple-element.40), channel_id=1, source_target_pairs={{0,4},{4,8},{8,12},{12,0},{1,5},{5,9},{9,13},{13,1},{2,6},{6,10},{... | collective-permute-start | bytes 98312 | tf_op jit(solution)/shard_map/ppermute | solution.py:28
  9.2 4.3 %collective-permute-start.2 = (f32[4,1,2,8,128]{4,3,2,1,0:T(8,128)S(1)}, f32[4,1,2,8,128]{4,3,2,1,0:T(8,128)S(1)}, u32[]{:S(2)}, u32[]{:S(2)}) collective-permute-start(f32[4,1,2,8,128]{4,3,2,1,0:T(8,128)S(1)} %get-tuple-element.41), channel_id=1, source_target_pairs={{0,12},{4,0},{8,4},{12,8},{1,13},{5,1},{9,5},{13,9},{2,14},{6,2},{... | collective-permute-start | bytes 98312 | tf_op jit(solution)/shard_map/ppermute | solution.py:28
  13.5 1.8 %copy-start.1 = (s32[2,2,2,128]{3,2,1,0:T(2,128)S(1)}, s32[2,2,2,128]{3,2,1,0:T(2,128)}, u32[]{:S(2)}) copy-start(s32[2,2,2,128]{3,2,1,0:T(2,128)} %act_ref.1) | copy-start | bytes 12292
  13.6 10.8 %collective-permute-start.3 = (f32[4,4,1,8,128]{4,3,2,1,0:T(8,128)S(1)}, f32[4,4,1,8,128]{4,3,2,1,0:T(8,128)S(1)}, u32[]{:S(2)}, u32[]{:S(2)}) collective-permute-start(f32[4,4,1,8,128]{4,3,2,1,0:T(8,128)S(1)} %get-tuple-element.32), channel_id=1, source_target_pairs={{0,1},{1,2},{2,3},{3,0},{4,5},{5,6},{6,7},{7,4},{8,9},{9,10},{10,1... | collective-permute-start | bytes 196616 | tf_op jit(solution)/shard_map/ppermute | solution.py:28
  13.6 4.7 %copy-start = (f32[2,2,2,128]{3,2,1,0:T(2,128)S(1)}, f32[2,2,2,128]{3,2,1,0:T(2,128)}, u32[]{:S(2)}) copy-start(f32[2,2,2,128]{3,2,1,0:T(2,128)} %len_ref.5) | copy-start | bytes 12292
  13.6 10.8 %collective-permute-start.4 = (f32[4,4,1,8,128]{4,3,2,1,0:T(8,128)S(1)}, f32[4,4,1,8,128]{4,3,2,1,0:T(8,128)S(1)}, u32[]{:S(2)}, u32[]{:S(2)}) collective-permute-start(f32[4,4,1,8,128]{4,3,2,1,0:T(8,128)S(1)} %get-tuple-element.33), channel_id=1, source_target_pairs={{0,3},{1,0},{2,1},{3,2},{4,7},{5,4},{6,5},{7,6},{8,11},{9,8},{10,9... | collective-permute-start | bytes 196616 | tf_op jit(solution)/shard_map/ppermute | solution.py:28
  44.8 3.3 %collective-permute-start.5 = (f32[4,4,1,4,128]{4,3,2,1,0:T(4,128)S(1)}, f32[4,4,1,4,128]{4,3,2,1,0:T(4,128)S(1)}, u32[]{:S(2)}, u32[]{:S(2)}) collective-permute-start(f32[4,4,1,4,128]{4,3,2,1,0:T(4,128)S(1)} %get-tuple-element.26), channel_id=1, source_target_pairs={{0,1},{1,2},{2,3},{3,0},{4,5},{5,6},{6,7},{7,4},{8,9},{9,10},{10,1... | collective-permute-start | bytes 98312 | tf_op jit(solution)/shard_map/ppermute | solution.py:28
  45.6 4.0 %collective-permute-start.6 = (f32[4,4,1,4,128]{4,3,2,1,0:T(4,128)S(1)}, f32[4,4,1,4,128]{4,3,2,1,0:T(4,128)S(1)}, u32[]{:S(2)}, u32[]{:S(2)}) collective-permute-start(f32[4,4,1,4,128]{4,3,2,1,0:T(4,128)S(1)} %get-tuple-element.27), channel_id=1, source_target_pairs={{0,3},{1,0},{2,1},{3,2},{4,7},{5,4},{6,5},{7,6},{8,11},{9,8},{10,9... | collective-permute-start | bytes 98312 | tf_op jit(solution)/shard_map/ppermute | solution.py:28
  49.6 17.6 %collective-permute-start.8 = (f32[4,1,2,4,128]{4,3,2,1,0:T(4,128)S(1)}, f32[4,1,2,4,128]{4,3,2,1,0:T(4,128)S(1)}, u32[]{:S(2)}, u32[]{:S(2)}) collective-permute-start(f32[4,1,2,4,128]{4,3,2,1,0:T(4,128)S(1)} %get-tuple-element.36), channel_id=1, source_target_pairs={{0,12},{4,0},{8,4},{12,8},{1,13},{5,1},{9,5},{13,9},{2,14},{6,2},{... | collective-permute-start | bytes 49160 | tf_op jit(solution)/shard_map/ppermute | solution.py:28
  65.8 5.5 %collective-permute-start.7 = (f32[4,1,2,4,128]{4,3,2,1,0:T(4,128)S(1)}, f32[4,1,2,4,128]{4,3,2,1,0:T(4,128)S(1)}, u32[]{:S(2)}, u32[]{:S(2)}) collective-permute-start(f32[4,1,2,4,128]{4,3,2,1,0:T(4,128)S(1)} %get-tuple-element.37), channel_id=1, source_target_pairs={{0,4},{4,8},{8,12},{12,0},{1,5},{5,9},{9,13},{13,1},{2,6},{6,10},{... | collective-permute-start | bytes 49160 | tf_op jit(solution)/shard_map/ppermute | solution.py:28
  71.3 5.5 %collective-permute-start.9 = (f32[2,2,2,4,128]{4,3,2,1,0:T(4,128)S(1)}, f32[2,2,2,4,128]{4,3,2,1,0:T(4,128)S(1)}, u32[]{:S(2)}, u32[]{:S(2)}) collective-permute-start(f32[2,2,2,4,128]{4,3,2,1,0:T(4,128)S(1)} %pad_maximum_fusion.5), channel_id=1, source_target_pairs={{0,16},{16,0},{1,17},{17,1},{2,18},{18,2},{3,19},{19,3},{4,20},{20... | collective-permute-start | bytes 49160 | tf_op jit(solution)/shard_map/ppermute | solution.py:28
